TPU v7x, 32 devices: a whole 2x2x4 slice. The times are simulated.
32 devices in a mesh: groups: 2 (over y), expert: 8 (over z, core), tensor: 2 (over x).
Axes of the slice: x: 2, y: 2, z: 4, core: 2. Of those that a mesh axis runs over, the one named last changes fastest.
Arguments:
- query: bfloat16 [768, 8192], P(('groups', 'expert'), 'tensor'), parts along dimension 0, may hold values from -40 to 40
- latest_key_value: bfloat16 [768, 2, 512], P(('groups', 'expert'), None, 'tensor'), parts along dimension 0, may hold values from -6 to 6
- cache: bfloat16 [768, 2, 128, 512], P(('groups', 'expert'), None, None, 'tensor'), parts along dimension 0, may hold values from -6 to 6
- lengths: int32 [768], P(('groups', 'expert')), parts along dimension 0, may hold values from 2 to 128
- w_out: bfloat16 [8192, 4096], P('tensor', 'expert'), may hold values from -0.0625 to 0.0625
- residual_in: bfloat16 [768, 4096], P(('groups', 'expert', 'tensor')), parts along dimension 0, may hold values from -6 to 6
- norm_gain: bfloat16 [4096], replicated, may hold values from 0.5 to 1.5
- expert_ids: int32 [768, 8], P(('groups', 'expert')), parts along dimension 0, may hold values from 0 to 15, all different within a row; in each aligned block of 48 rows (0 to 47, 48 to 95, ...) at most 48 rows name the same one
- route_weights: float32 [768, 8], P(('groups', 'expert')), parts along dimension 0, may hold values from 0.05 to 0.5
- w_gate: bfloat16 [16, 4096, 768], P('expert', None, 'tensor'), may hold values from -0.09375 to 0.09375
- w_up: bfloat16 [16, 4096, 768], P('expert', None, 'tensor'), may hold values from -0.09375 to 0.09375
- w_down: bfloat16 [16, 768, 4096], P('expert', 'tensor'), may hold values from -0.21875 to 0.21875
Outputs:
- layer_out: bfloat16 [768, 4096], P(('groups', 'expert', 'tensor')), parts along dimension 0
There are 2 independent parts, one for each index of `groups`. A program takes and returns all parts, laid end to end along the dimension named above; an argument that names none is the same for every part. Nothing has to cross between parts.
Inputs may be any that keep to these rules, and one draw needn't show every extreme that they name: `expert_ids`: the 8 entries of a row differ. Within each aligned block of 48 rows (the rows of one index of the expert axis) no expert is named by more than 48 rows, and in every draw some block reaches that bound.
All inputs are finite; a program needn't handle non-finite values.
Results may differ from a plain program's by a relative error of at most 0.0095.
Values may be sent and summed in bfloat16 or wider, within the bound.
No kernel may reach another device: no remote copies, remote signals or barrier semaphores. Data moves between devices by JAX's collectives and lax.ppermute only.
A program may use at most 128 MiB of HBM per device.

v0:
```python
import math

import jax
import jax.numpy as jnp
from jax import lax
from jax.sharding import PartitionSpec as P

HEAD_SIZE = 128


def attention(query, latest_key_value, cache, lengths):
    token_count = query.shape[0]
    kv_heads = latest_key_value.shape[2] // HEAD_SIZE
    group_size = query.shape[1] // (kv_heads * HEAD_SIZE)
    positions = cache.shape[2]
    factor = 1.0 / math.sqrt(HEAD_SIZE)
    queries = query.reshape(token_count, kv_heads, group_size, HEAD_SIZE)
    cached_keys = cache[:, 0].reshape(token_count, positions, kv_heads, HEAD_SIZE)
    cached_values = cache[:, 1].reshape(token_count, positions, kv_heads, HEAD_SIZE)
    fresh_keys = latest_key_value[:, 0].reshape(token_count, kv_heads, HEAD_SIZE)
    fresh_values = (
        latest_key_value[:, 1].reshape(token_count, kv_heads, HEAD_SIZE).astype(jnp.float32)
    )
    scores = (
        jnp.einsum("tkgd,tlkd->tkgl", queries, cached_keys, preferred_element_type=jnp.float32)
        * factor
    )
    valid = jnp.arange(positions, dtype=jnp.int32)[None, :] < lengths[:, None]
    scores = jnp.where(valid[:, None, None, :], scores, -jnp.inf)
    own_score = (
        jnp.einsum("tkgd,tkd->tkg", queries, fresh_keys, preferred_element_type=jnp.float32)
        * factor
    )
    highest = jnp.maximum(jnp.max(scores, axis=-1), own_score)
    weights = jnp.exp(scores - highest[..., None])
    own_weight = jnp.exp(own_score - highest)
    total = jnp.sum(weights, axis=-1) + own_weight
    probs = (weights / total[..., None]).astype(jnp.bfloat16)
    own_prob = lax.optimization_barrier((own_weight / total).astype(jnp.bfloat16))
    mixed = jnp.einsum("tkgl,tlkd->tkgd", probs, cached_values, preferred_element_type=jnp.float32)
    mixed = mixed + own_prob.astype(jnp.float32)[..., None] * fresh_values[:, :, None, :]
    return mixed.reshape(token_count, -1).astype(jnp.bfloat16)


def per_device(
    query,
    latest_key_value,
    cache,
    lengths,
    w_out,
    residual_in,
    norm_gain,
    expert_ids,
    route_weights,
    w_gate,
    w_up,
    w_down,
):
    attended = attention(query, latest_key_value, cache, lengths)
    projected = jnp.dot(
        lax.all_gather(attended, "expert", axis=0, tiled=True),
        w_out,
        preferred_element_type=jnp.float32,
    )
    expert_groups = lax.axis_size("expert")
    token_count = query.shape[0]
    column_count = w_out.shape[1]
    grouped = projected.reshape(expert_groups, token_count, column_count)
    summed = lax.psum_scatter(
        grouped.astype(jnp.bfloat16), "tensor", scatter_dimension=1, tiled=True
    ).astype(jnp.float32)
    own_rows = lax.all_to_all(
        summed.astype(jnp.bfloat16), "expert", split_axis=0, concat_axis=2, tiled=True
    ).astype(summed.dtype)
    stream = residual_in.astype(jnp.float32) + own_rows.reshape(residual_in.shape)
    meansq = jnp.mean(stream * stream, axis=-1, keepdims=True)
    normed = (stream * lax.rsqrt(meansq + 1e-06) * norm_gain.astype(jnp.float32)).astype(
        jnp.bfloat16
    )
    choose_count = expert_ids.shape[1]
    local_experts = w_gate.shape[0]
    expert_total = local_experts * expert_groups
    capacity = min(token_count, 2 * token_count * choose_count // expert_total)
    slot_total = expert_total * capacity
    flat_ids = expert_ids.reshape(-1)
    onehot = (flat_ids[:, None] == jnp.arange(expert_total, dtype=jnp.int32)[None, :]).astype(
        jnp.int32
    )
    earlier = jnp.cumsum(onehot, axis=0) - onehot
    slot_index = jnp.sum(earlier * onehot, axis=1)
    target = (flat_ids * capacity + slot_index).reshape(token_count, choose_count)
    matches = target[:, :, None] == jnp.arange(slot_total, dtype=jnp.int32)[None, None, :]
    selector = jnp.any(matches, axis=1).astype(jnp.bfloat16)
    mixing = jnp.sum(jnp.where(matches, route_weights[:, :, None], 0.0), axis=1)
    contract = (((0,), (0,)), ((), ()))
    whole_rows = lax.all_gather(normed, "tensor", axis=0, tiled=True)
    packed = lax.dot_general(selector, whole_rows, contract, preferred_element_type=jnp.float32)
    packed = packed.astype(jnp.bfloat16).reshape(expert_total, capacity, -1)
    arrived = lax.all_to_all(packed, "expert", split_axis=0, concat_axis=1, tiled=True)
    gate_proj = jnp.einsum("xsd,xdf->xsf", arrived, w_gate, preferred_element_type=jnp.float32)
    up_proj = jnp.einsum("xsd,xdf->xsf", arrived, w_up, preferred_element_type=jnp.float32)
    activated = (jax.nn.silu(gate_proj) * up_proj).astype(jnp.bfloat16)
    partial_out = jnp.einsum("xsf,xfd->xsd", activated, w_down, preferred_element_type=jnp.float32)
    expert_out = lax.psum_scatter(
        partial_out.astype(jnp.bfloat16), "tensor", scatter_dimension=2, tiled=True
    )
    returned = lax.all_to_all(expert_out, "expert", split_axis=1, concat_axis=0, tiled=True)
    mixture = jnp.dot(
        mixing,
        returned.reshape(slot_total, -1).astype(jnp.float32),
        precision=lax.Precision.HIGHEST,
    )
    mixture_rows = lax.all_to_all(
        mixture.astype(jnp.bfloat16), "tensor", split_axis=0, concat_axis=1, tiled=True
    ).astype(mixture.dtype)
    return (stream + mixture_rows).astype(jnp.bfloat16)


def solution(mesh):
    placed = (
        P(("groups", "expert"), "tensor"),
        P(("groups", "expert"), None, "tensor"),
        P(("groups", "expert"), None, None, "tensor"),
        P(("groups", "expert")),
        P("tensor", "expert"),
        P(("groups", "expert", "tensor"), None),
        P(),
        P(("groups", "expert"), None),
        P(("groups", "expert"), None),
        P("expert", None, "tensor"),
        P("expert", None, "tensor"),
        P("expert", "tensor", None),
    )
    return jax.shard_map(
        per_device,
        mesh=mesh,
        in_specs=placed,
        out_specs=P(("groups", "expert", "tensor"), None),
        check_vma=False,
    )
```

profile of v0, /device:TPU:0, one launch (start us, length us, event | category | flops | bytes accessed | tf_op | source)
XLA Modules:
  0.0 453.0 jit_solution(3351646385357858465)
XLA Ops:
  6.5 6.3 %fusion.17 = (bf16[48,1,128,256]{3,2,1,0:T(8,128)(2,1)}, bf16[48,1,128,256]{3,2,1,0:T(8,128)(2,1)}) fusion(bf16[48,2,128,256]{3,2,1,0:T(8,128)(2,1)} %param.14), kind=kLoop, calls=%fused_computation.47 | loop fusion | bytes 12582912 | tf_op jit(solution)/shard_map/slice | solution.py:18
  12.8 3.5 copy.99
  16.5 0.9 slice_convert_fusion
  17.4 1.1 fusion.8
  18.5 1.1 fusion.18
  19.6 0.8 copy-done.1
  20.4 0.6 fusion.4
  21.2 4.8 %copy.100 = bf16[48,1,128,256]{2,3,0,1:T(8,128)(2,1)} copy(bf16[48,1,128,256]{3,2,1,0:T(8,128)(2,1)} %get-tuple-element.6) | data formatting | bytes 6291456
  25.9 3.7 fusion.2
  29.6 0.9 copy.112
  30.6 41.0 %all-gather.2.cloned.1.call-done = bf16[384,4096]{1,0:T(8,128)(2,1)} async-done(((bf16[48,4096]{1,0:T(8,128)(2,1)}), bf16[384,4096]{1,0:T(8,128)(2,1)}) %all-gather.2.cloned.1.call-update) | async-done | bytes 3145744 | tf_op jit(solution)/shard_map/all_gather | solution.py:61
  71.6 4.9 %convolution_convert_fusion.3 = bf16[384,512]{1,0:T(8,128)(2,1)S(1)} fusion(bf16[384,4096]{1,0:T(8,128)(2,1)} %all-gather.2.cloned.1.call-done, bf16[4096,512]{1,0:T(8,128)(2,1)} %param.16), kind=kOutput, calls=%fused_computation.9 | convolution fusion | flops 1610809344 | bytes 7733248 | tf_op jit(solution)/shard_map/dot_general | solution.py:60
  76.6 0.8 copy.105
  77.4 0.1 copy.82
  77.5 0.1 eq.42
  77.6 0.1 eq.38
  77.7 0.9 reduce-window.6
  78.6 0.2 slice_reduce_fusion
  78.8 0.1 fusion.13
  78.9 0.1 reduce_sum.40
  79.1 10.6 %reduce-scatter.7.cloned.1.call-done = bf16[24,4096]{1,0:T(8,128)(2,1)} async-done(((bf16[48,4096]{1,0:T(8,128)(2,1)}), bf16[24,4096]{1,0:T(8,128)(2,1)}) %reduce-scatter.7.cloned.1.call-update) | async-done | bytes 196624
  89.6 1.0 copy.106
  90.6 0.7 copy.98
  91.3 4.6 %all-to-all-start = ((bf16[8,24,512]{2,1,0:T(8,128)(2,1)}), bf16[8,24,512]{2,1,0:T(8,128)(2,1)S(1)}, u32[]{:S(2)}, u32[]{:S(2)}) async-start(bf16[8,24,512]{2,1,0:T(8,128)(2,1)} %copy.98), calls=%async_computation | async-start | bytes 393216 | tf_op jit(solution)/shard_map/all_to_all | solution.py:72
  96.1 0.4 fusion.3
  96.5 0.2 copy-done.7
  96.7 7.6 %all-to-all-done = bf16[8,24,512]{2,1,0:T(8,128)(2,1)S(1)} async-done(((bf16[8,24,512]{2,1,0:T(8,128)(2,1)}), bf16[8,24,512]{2,1,0:T(8,128)(2,1)S(1)}, u32[]{:S(2)}, u32[]{:S(2)}) %all-to-all-start) | async-done | bytes 196640 | tf_op jit(solution)/shard_map/all_to_all | solution.py:72
  104.4 0.2 multiply_reduce_fusion
  104.5 0.1 multiply_convert_fusion
  104.7 6.3 %all_gather.7 = bf16[48,4096]{1,0:T(8,128)(2,1)S(1)} all-gather(bf16[24,4096]{1,0:T(8,128)(2,1)S(1)} %multiply_convert_fusion), channel_id=1, replica_groups=mesh['groups'=2,'expert'=8,'tensor'=2] {'tensor'}, dimensions={0}, use_global_device_ids=true | all-gather | bytes 589824 | tf_op jit(solution)/shard_map/all_gather | solution.py:96
  111.0 1.8 convolution_convert_fusion
  112.9 142.7 %all_to_all.55 = bf16[16,48,4096]{2,1,0:T(8,128)(2,1)S(1)} all-to-all(bf16[16,48,4096]{2,1,0:T(8,128)(2,1)S(1)} %bitcast.89), channel_id=1, replica_groups=mesh['groups'=2,'expert'=8,'tensor'=2] {'expert'}, dimensions={0} | all-to-all | bytes 12582912 | tf_op jit(solution)/shard_map/all_to_all | solution.py:99
  255.6 0.8 copy.88
  256.4 2.7 copy-done
  259.1 4.5 fusion.20
  263.5 12.6 %convolution_convert_fusion.1 = bf16[2,384,4096]{2,1,0:T(8,128)(2,1)} fusion(bf16[2,384,4096]{2,1,0:T(8,128)(2,1)} %param.23, bf16[2,384,4096]{2,1,0:T(8,128)(2,1)} %bitcast.95, bf16[2,4096,384]{2,1,0:T(8,128)(2,1)} %param.22, f32[2,384,384]{2,1,0:T(8,128)} %fusion.20), kind=kOutput, calls=%fused_computation.1 | convolution fusion | flops 4836753408 | bytes 26345472 | tf_op jit(solution)/shard_map/xsf,xfd->xsd/dot_general | solution.py:103
  276.2 75.3 %reduce-scatter.5.cloned.1.call-done = bf16[2,384,2048]{2,1,0:T(8,128)(2,1)} async-done(((bf16[2,384,4096]{2,1,0:T(8,128)(2,1)}), bf16[2,384,2048]{2,1,0:T(8,128)(2,1)}) %reduce-scatter.5.cloned.1.call-update) | async-done | bytes 3145744 | tf_op jit(solution)/shard_map/reduce_scatter | solution.py:104
  351.4 6.8 %copy.89 = bf16[2,384,2048]{2,0,1:T(2,128)(2,1)} copy(bf16[2,384,2048]{2,1,0:T(8,128)(2,1)} %reduce-scatter.5.cloned.1.call-done) | data formatting | bytes 6291456 | tf_op jit(solution)/shard_map/reduce_scatter | solution.py:104
  358.2 4.7 %all-to-all-start.2 = ((bf16[2,384,2048]{2,0,1:T(2,128)(2,1)}), bf16[2,384,2048]{2,0,1:T(2,128)(2,1)S(1)}, u32[]{:S(2)}, u32[]{:S(2)}) async-start(bf16[2,384,2048]{2,0,1:T(2,128)(2,1)} %copy.89), calls=%async_computation.3 | async-start | bytes 6291456 | tf_op jit(solution)/shard_map/all_to_all | solution.py:107
  363.0 0.7 copy.87
  363.6 1.9 select_reduce_fusion
  365.5 69.0 %all-to-all-done.2 = bf16[2,384,2048]{2,0,1:T(2,128)(2,1)S(1)} async-done(((bf16[2,384,2048]{2,0,1:T(2,128)(2,1)}), bf16[2,384,2048]{2,0,1:T(2,128)(2,1)S(1)}, u32[]{:S(2)}, u32[]{:S(2)}) %all-to-all-start.2) | async-done | bytes 3145760 | tf_op jit(solution)/shard_map/all_to_all | solution.py:107
  434.5 1.4 copy.90
  435.8 0.4 copy.91
  436.3 0.5 copy-done.5
  436.7 1.7 convolution_convert_fusion.2
  438.5 7.2 %all_to_all.56 = bf16[2,24,2048]{2,1,0:T(8,128)(2,1)S(1)} all-to-all(bf16[2,24,2048]{2,1,0:T(8,128)(2,1)S(1)} %bitcast.106), channel_id=1, replica_groups=mesh['groups'=2,'expert'=8,'tensor'=2] {'tensor'}, dimensions={0} | all-to-all | bytes 393216 | tf_op jit(solution)/shard_map/all_to_all | solution.py:113
  445.7 0.8 add_convert_fusion
  (47 shorter events, 0.8 us)
Async XLA Ops:
  6.5 65.1 %all-gather.2.cloned.1.call-start = ((), (), s32[]{:S(2)}) async-start(), calls=%async_computation.6 | async-start | bytes 3538944 | tf_op jit(solution)/shard_map/all_gather | solution.py:61
  12.8 3.5 copy-start.6
  12.8 3.6 copy-start.11
  19.5 0.9 copy-start.1
  21.1 4.8 %copy-start.2 = (f32[48,2,16,128]{3,2,1,0:T(8,128)S(1)}, f32[48,2,16,128]{3,2,1,0:T(8,128)}, u32[]{:S(2)}) copy-start(f32[48,2,16,128]{3,2,1,0:T(8,128)} %copy-done.1) | copy-start | bytes 2359300
  30.5 46.8 %copy-start.8 = (s32[48,8]{0,1:T(8,128)S(1)}, s32[48,8]{0,1:T(8,128)}, u32[]{:S(2)}) copy-start(s32[48,8]{0,1:T(8,128)} %param.19) | copy-start | bytes 4612
  30.5 47.1 %copy-start.9 = (bf16[4096]{0:T(1024)(128)(2,1)S(1)}, bf16[4096]{0:T(1024)(128)(2,1)}, u32[]{:S(2)}) copy-start(bf16[4096]{0:T(1024)(128)(2,1)} %param.18) | copy-start | bytes 24580
  30.6 59.1 %reduce-scatter.7.cloned.1.call-start = ((), (), s32[]{:S(2)}) async-start(), calls=%async_computation.8 | async-start | bytes 589824
  76.6 27.8 %copy-start.3 = (bf16[24,4096]{1,0:T(8,128)(2,1)S(1)}, bf16[24,4096]{1,0:T(8,128)(2,1)}, u32[]{:S(2)}) copy-start(bf16[24,4096]{1,0:T(8,128)(2,1)} %param.17) | copy-start | bytes 589828
  91.3 12.9 %all-to-all-start = ((bf16[8,24,512]{2,1,0:T(8,128)(2,1)}), bf16[8,24,512]{2,1,0:T(8,128)(2,1)S(1)}, u32[]{:S(2)}, u32[]{:S(2)}) async-start(bf16[8,24,512]{2,1,0:T(8,128)(2,1)} %copy.98), calls=%async_computation | async-start | bytes 393216 | tf_op jit(solution)/shard_map/all_to_all | solution.py:72
  96.0 255.5 %reduce-scatter.5.cloned.1.call-start = ((), (), s32[]{:S(2)}) async-start(), calls=%async_computation.7 | async-start | bytes 9437184 | tf_op jit(solution)/shard_map/reduce_scatter | solution.py:104
  96.1 0.6 copy-start.7
  112.8 146.2 %slice-start = ((s8[6291456]{0:T(1024)(128)(4,1)}), s8[4194304]{0:T(1024)(128)(4,1)S(1)}, s32[]{:S(2)}) async-start(s8[6291456]{0:T(1024)(128)(4,1)} %bitcast.115), calls=%async_computation.9 | async-start | bytes 8388608
  255.6 3.5 slice-start.1
  256.4 2.7 copy-start
  358.2 4.7 %copy-start.10 = (f32[48,8]{0,1:T(8,128)S(1)}, f32[48,8]{0,1:T(8,128)}, u32[]{:S(2)}) copy-start(f32[48,8]{0,1:T(8,128)} %param.20) | copy-start | bytes 4612
  358.2 76.2 %all-to-all-start.2 = ((bf16[2,384,2048]{2,0,1:T(2,128)(2,1)}), bf16[2,384,2048]{2,0,1:T(2,128)(2,1)S(1)}, u32[]{:S(2)}, u32[]{:S(2)}) async-start(bf16[2,384,2048]{2,0,1:T(2,128)(2,1)} %copy.89), calls=%async_computation.3 | async-start | bytes 6291456 | tf_op jit(solution)/shard_map/all_to_all | solution.py:107
  435.8 0.9 copy-start.5
  436.3 9.5 %copy-start.4 = (bf16[24,4096]{1,0:T(8,128)(2,1)S(1)}, bf16[24,4096]{1,0:T(8,128)(2,1)}, u32[]{:S(2)}) copy-start(bf16[24,4096]{1,0:T(8,128)(2,1)} %param.17) | copy-start | bytes 589828
Sparse Core Ops, SparseCore 0:
  30.7 40.9 all-gather.1
  77.5 12.0 reduce-scatter.6
  276.3 75.0 reduce-scatter.4
where the time goes:
time: 454 us; the launch traced here: 453 us
  waiting for transfers between devices  203 us (45%)
  blocking collectives  156 us (34%)
  local copies, waits for them, and re-layouts  33 us (7%)
  matrix products  31.4 us (7%)
  between operations  13.4 us (3%)
  starting transfers between devices  9.44 us (2%)
  other arithmetic  6.05 us (1%)
    all_to_all x1, blocking collectives, per_device(): lax.all_to_all(packed, 'expert', split_axis=0, concat_axis=1, tiled=True)  143 us
    reduce_scatter x1, waiting for transfers between devices, per_device(): lax.psum_scatter(partial_out.astype(jnp.bfloat16), 'tensor', scatter_dime...  75.3 us
    all_to_all x1, waiting for transfers between devices, per_device(): lax.all_to_all(expert_out, 'expert', split_axis=1, concat_axis=0, tiled=T...  69 us
    all_gather x1, waiting for transfers between devices, per_device(): lax.all_gather(attended, 'expert', axis=0, tiled=True)  41 us
    unnamed x38, local copies, waits for them, and re-layouts  16.8 us
    dot_general x1, matrix products, per_device(): jnp.einsum('xsf,xfd->xsd', activated, w_down, preferred_element_type=jnp....  12.6 us
    unnamed x4, waiting for transfers between devices  10.6 us
  transfers between devices with their start and end apart: 5, of which 5 were waited for; matrix products, arithmetic and copies ran while one was open for 1% of the time, Pallas kernels for 0%

commit v1 on v0

v1 whole, which is shorter than its diff:
```python
import functools
import math

import jax
import jax.numpy as jnp
from jax import lax
from jax.experimental import pallas as pl
from jax.experimental.pallas import tpu as pltpu
from jax.sharding import PartitionSpec as P

HEAD_SIZE = 128
CORES = 2
BF16 = jnp.bfloat16
F32 = jnp.float32


NT = (((1,), (1,)), ((), ()))


def fold_order(count):
    return list(range(0, count, 2)) + list(range(count - 1 - count % 2, 0, -2))


def chip_perm(chips, shift):
    order = fold_order(chips)
    place = {z: i for i, z in enumerate(order)}
    to = lambda z: order[(place[z] + shift) % chips]
    return [(z * CORES + c, to(z) * CORES + c) for z in range(chips) for c in range(CORES)]


def core_perm(chips):
    return [(z * CORES + c, z * CORES + 1 - c) for z in range(chips) for c in range(CORES)]


def chip_table(chips, sign):
    order = fold_order(chips)
    place = {z: i for i, z in enumerate(order)}
    return [[order[(place[z] + sign * s) % chips] for s in range(chips)] for z in range(chips)]


def chip_send(piece, chips, shift):
    return lax.ppermute(piece, "expert", chip_perm(chips, shift))


def core_swap(piece, chips):
    return lax.ppermute(piece, "expert", core_perm(chips))


def tensor_shift(piece, tensors, shift):
    return lax.ppermute(piece, "tensor", [((i + shift) % tensors, i) for i in range(tensors)])


def chip_gather(piece, chips):
    pieces = [None] * chips
    pieces[0] = piece
    ahead = back = piece
    for s in range(1, chips // 2 + 1):
        if pieces[s] is None:
            ahead = chip_send(ahead, chips, 1)
            pieces[s] = ahead
        if pieces[chips - s] is None:
            back = chip_send(back, chips, -1)
            pieces[chips - s] = back
    return pieces


def chip_scatter(take, chips):
    total = take(0)
    for sign, steps in ((1, chips // 2), (-1, (chips - 1) // 2)):
        held = None
        for s in range(steps, 0, -1):
            own = take(s if sign > 0 else chips - s)
            held = own if held is None else own + held
            held = chip_send(held.astype(BF16), chips, sign)
            held = held.astype(F32)
        if held is not None:
            total = total + held
    return total


def attention_kernel(
    chunk, kv_heads, head_count, tab_ref, len_ref, q_ref, new_ref, cache_ref, out_ref, qs, buf, sems
):
    rows = q_ref.shape[1]
    group = head_count // kv_heads
    factor = 1.0 / math.sqrt(HEAD_SIZE)
    first = tab_ref[0] * rows
    pitch = qs.shape[0] // rows

    copies = []
    for c in range(rows // chunk):
        copies.append(
            pltpu.make_async_copy(
                cache_ref.at[pl.ds(first + c * chunk, chunk)],
                buf.at[pl.ds(c * chunk, chunk)],
                sems.at[c],
            )
        )
        copies[-1].start()
    for h in range(head_count):
        qs[pl.ds(h, rows, stride=pitch), :] = q_ref[
            0, :, h * HEAD_SIZE : (h + 1) * HEAD_SIZE
        ].astype(F32)

    positions = buf.shape[2]
    block = chunk * head_count
    pos = lax.broadcasted_iota(jnp.int32, (head_count, positions), 1)
    head_kv = lax.broadcasted_iota(jnp.int32, (block, HEAD_SIZE), 0) // group % kv_heads
    wide = (head_count, new_ref.shape[3])
    for c in range(rows // chunk):
        span = range(c * chunk, (c + 1) * chunk)
        q32 = jnp.concatenate([qs[t * pitch : t * pitch + head_count, :] for t in span], axis=0)
        spread = [jnp.where(head_kv == kv, q32, 0.0) for kv in range(kv_heads)]
        q = spread[0] if kv_heads == 1 else jnp.concatenate(spread, axis=1)
        q16 = q.astype(BF16)
        keys = [jnp.broadcast_to(new_ref[0, t, 0:1, :].astype(F32), wide) for t in span]
        values = [jnp.broadcast_to(new_ref[0, t, 1:2, :].astype(F32), wide) for t in span]
        own = jnp.sum(q * jnp.concatenate(keys, axis=0), axis=1, keepdims=True) * factor
        copies[c].wait()
        scores = []
        for i, t in enumerate(span):
            score = lax.dot_general(
                q16[i * head_count : (i + 1) * head_count],
                buf[t, 0],
                NT,
                preferred_element_type=F32,
            )
            scores.append(jnp.where(pos < len_ref[first + t], score * factor, -jnp.inf))
        scores = jnp.concatenate(scores, axis=0)
        highest = jnp.maximum(jnp.max(scores, axis=1, keepdims=True), own)
        weights = jnp.exp(scores - highest)
        own_weight = jnp.exp(own - highest)
        inverse = 1.0 / (jnp.sum(weights, axis=1, keepdims=True) + own_weight)
        probs = (weights * inverse).astype(BF16)
        own_prob = (own_weight * inverse).astype(BF16).astype(F32)
        mixed = jnp.concatenate(
            [
                jnp.dot(
                    probs[i * head_count : (i + 1) * head_count],
                    buf[t, 1],
                    preferred_element_type=F32,
                )
                for i, t in enumerate(span)
            ],
            axis=0,
        )
        mixed = mixed + own_prob * jnp.concatenate(values, axis=0)
        out = mixed[:, :HEAD_SIZE]
        for kv in range(1, kv_heads):
            out = jnp.where(head_kv == kv, mixed[:, kv * HEAD_SIZE : (kv + 1) * HEAD_SIZE], out)
        for i, t in enumerate(span):
            qs[t * pitch : t * pitch + head_count, :] = out[i * head_count : (i + 1) * head_count]

    for h in range(head_count):
        out_ref[:, h * HEAD_SIZE : (h + 1) * HEAD_SIZE] = qs[
            pl.ds(h, rows, stride=pitch), :
        ].astype(BF16)


def attend(part, query, latest, cache, lengths, parts):
    token_count, width = query.shape
    rows = token_count // parts
    kv_width = latest.shape[2]
    kv_heads = kv_width // HEAD_SIZE
    head_count = width // HEAD_SIZE
    chunk = next(k for k in (8, 6, 4, 3, 2, 1) if rows % k == 0)
    return pl.pallas_call(
        functools.partial(attention_kernel, chunk, kv_heads, head_count),
        grid_spec=pltpu.PrefetchScalarGridSpec(
            num_scalar_prefetch=2,
            grid=(1,),
            in_specs=[
                pl.BlockSpec((1, rows, width), lambda i, tab, ln: (tab[0], 0, 0)),
                pl.BlockSpec((1, rows, 2, kv_width), lambda i, tab, ln: (tab[0], 0, 0, 0)),
                pl.BlockSpec(memory_space=pltpu.HBM),
            ],
            out_specs=pl.BlockSpec((rows, width), lambda i, tab, ln: (0, 0)),
            scratch_shapes=[
                pltpu.VMEM((rows * (head_count + 8), HEAD_SIZE), F32),
                pltpu.VMEM((rows,) + cache.shape[1:], BF16),
                pltpu.SemaphoreType.DMA((rows // chunk,)),
            ],
        ),
        out_shape=jax.ShapeDtypeStruct((rows, width), BF16),
        compiler_params=pltpu.CompilerParams(
            dimension_semantics=("arbitrary",), vmem_limit_bytes=12 << 20
        ),
        name="attend",
    )(
        part.reshape(1),
        lengths,
        *in_hbm(
            query.reshape(parts, rows, width), latest.reshape(parts, rows, 2, kv_width), cache
        ),
    )


def in_hbm(*arrays):
    return [pltpu.with_memory_space_constraint(a, pltpu.HBM) for a in arrays]


def project_kernel(count, steps, tab_ref, *refs):
    pieces, w_ref, adds, out_ref, buf, sems = (
        refs[:count],
        refs[count],
        refs[count + 1 : -3],
        refs[-3],
        refs[-2],
        refs[-1],
    )
    rows, width = pieces[0].shape
    columns = w_ref.shape[1]
    deep = width // steps
    copies = [
        pltpu.make_async_copy(
            w_ref.at[pl.ds(k * deep, deep)], buf.at[pl.ds(k * deep, deep)], sems.at[k]
        )
        for k in range(steps)
    ]
    for copy in copies:
        copy.start()
    result = None
    for k in range(steps):
        span = slice(k * deep, (k + 1) * deep)
        lhs = jnp.concatenate([p[:, span].astype(F32) for p in pieces], axis=0).astype(BF16)
        copies[k].wait()
        term = jnp.dot(lhs, buf[span, :], preferred_element_type=F32)
        result = term if result is None else result + term
    for i in range(count):
        block = tab_ref[i]
        value = result[i * rows : (i + 1) * rows]
        for a in adds:
            value = value + a[block][:, :columns].astype(F32)
        out_ref[block] = value.astype(BF16)


def project(table, pieces, w_out, adds):
    rows, _ = pieces[0].shape
    count = len(pieces)
    steps = 4
    vmem = pl.BlockSpec(memory_space=pltpu.VMEM)
    hbm = pl.BlockSpec(memory_space=pltpu.HBM)
    return pl.pallas_call(
        functools.partial(project_kernel, count, steps),
        in_specs=[pl.BlockSpec(memory_space=pltpu.SMEM)]
        + [vmem] * count
        + [hbm]
        + [vmem] * len(adds),
        out_specs=vmem,
        out_shape=jax.ShapeDtypeStruct((count, rows, w_out.shape[1]), BF16),
        scratch_shapes=[
            pltpu.VMEM(w_out.shape, BF16),
            pltpu.SemaphoreType.DMA((steps,)),
        ],
        compiler_params=pltpu.CompilerParams(vmem_limit_bytes=16 << 20),
        name="project",
    )(table, *pieces, *in_hbm(w_out), *adds)


def load_down(wd_ref, wd_buf, sem, first):
    columns = wd_buf.shape[2]
    return pltpu.make_async_copy(wd_ref.at[:, :, pl.ds(first, columns)], wd_buf, sem)


def down_product(acts, wd_buf, tab_ref, send_ref, keep_ref):
    local, hidden, columns = wd_buf.shape
    chips = acts[0].shape[1]
    count = chips * CORES
    core = tab_ref[count + 1]
    block = min(columns, 1024)
    aligned = hidden % 128 == 0
    for out_ref, half in ((send_ref, 1 - core), (keep_ref, core)):
        lhs = []
        for e in range(local):
            picked = [
                act[e, tab_ref[count + 2 + s], half].astype(F32)
                for act in acts
                for s in range(chips)
            ]
            lhs.append(jnp.concatenate(picked, axis=0).astype(BF16))
        if aligned:
            lhs = [jnp.concatenate(lhs, axis=1)]
        for b in range(columns // block):
            span = slice(b * block, (b + 1) * block)
            if aligned:
                right = [wd_buf[:, :, span].reshape(local * hidden, block)]
            else:
                right = [wd_buf[e, :, span] for e in range(local)]
            result = sum(jnp.dot(l, r, preferred_element_type=F32) for l, r in zip(lhs, right))
            out_ref[:, :, :, span] = result.astype(BF16).reshape(out_ref.shape[:3] + (block,))


def up_kernel(part, last, count, tab_ref, *refs):
    refs = list(refs)
    slices = [refs.pop(0) for _ in range(count)]
    gain_ref, weight_ref, wg_ref, wu_ref = [refs.pop(0) for _ in range(4)]
    acts = [refs.pop(0) for _ in range(part)] if last else []
    wd_ref = refs.pop(0) if last else None
    act_ref = refs.pop(0)
    own_ref = refs.pop(0) if part == 0 else None
    send_ref, keep_ref = (refs.pop(0), refs.pop(0)) if last else (None, None)
    wg_buf, wu_buf, sems = [refs.pop(0) for _ in range(3)]
    local, features, hidden = wg_ref.shape
    _, rows, columns = slices[0].shape
    total = count * rows
    aligned = hidden % 128 == 0

    def span_of(i):
        return pl.ds(pl.multiple_of(tab_ref[i] * columns, columns), columns)

    copies = [
        [
            pltpu.make_async_copy(src.at[:, span_of(i), :], dst.at[:, span_of(i), :], sems.at[k, i])
            for k, (src, dst) in enumerate(((wg_ref, wg_buf), (wu_ref, wu_buf)))
        ]
        for i in range(count)
    ]
    for pair in copies:
        for copy in pair:
            copy.start()
    if last:
        down = load_down(wd_ref, refs[0], refs[1].at[0], 0)
        down.start()
    squares = jnp.zeros((total, 1), F32)
    sums = None
    for i in range(count):
        span = span_of(i)
        if part == 0:
            own_ref[:, span] = slices[i][tab_ref[count]]
        x = slices[i][...].astype(F32).reshape(total, columns)
        squares = squares + jnp.sum(x * x, axis=1, keepdims=True)
        scaled = (x * gain_ref[:, span].astype(F32)).astype(BF16)
        for copy in copies[i]:
            copy.wait()
        weights = [w[e, span, :] for w in (wg_buf, wu_buf) for e in range(local)]
        if aligned:
            weights = [jnp.concatenate(weights, axis=1)]
        more = [jnp.dot(scaled, w, preferred_element_type=F32) for w in weights]
        sums = more if sums is None else [a + b for a, b in zip(sums, more)]
    if aligned:
        sums = [sums[0][:, k * hidden : (k + 1) * hidden] for k in range(2 * local)]
    scale = lax.rsqrt(squares * (1.0 / features) + 1e-06)
    for e in range(local):
        gate = sums[e] * scale
        up = sums[local + e] * scale
        chosen = weight_ref[part, :, e : e + 1]
        value = gate / (1.0 + jnp.exp(-gate)) * up * chosen
        value = jnp.where(chosen != 0.0, value, 0.0).astype(BF16)
        for i in range(count):
            act_ref[e, i // CORES, i % CORES] = value[i * rows : (i + 1) * rows]
    if last:
        down.wait()
        down_product(acts + [act_ref], refs[0], tab_ref, send_ref, keep_ref)


def expert_up(table, part, slices, gain, weights, w_gate, w_up, acts=None, w_down=None, pieces=1):
    count = len(slices)
    local, features, hidden = w_gate.shape
    _, rows, _ = slices[0].shape
    chips = count // CORES
    vmem = pl.BlockSpec(memory_space=pltpu.VMEM)
    hbm = pl.BlockSpec(memory_space=pltpu.HBM)
    last = w_down is not None
    shapes = [jax.ShapeDtypeStruct((local, chips, CORES, rows, hidden), BF16)]
    if part == 0:
        shapes.append(jax.ShapeDtypeStruct((rows, features), BF16))
    specs = [pl.BlockSpec(memory_space=pltpu.SMEM)] + [vmem] * (count + 2) + [hbm] * 2
    operands = [table, *slices, gain.reshape(1, -1), weights, *in_hbm(w_gate, w_up)]
    scratch = [
        pltpu.VMEM(w_gate.shape, BF16),
        pltpu.VMEM(w_up.shape, BF16),
        pltpu.SemaphoreType.DMA((2, count)),
    ]
    if last:
        wide = features // pieces
        shapes += [jax.ShapeDtypeStruct((part + 1, chips, rows, wide), BF16)] * 2
        specs += [vmem] * part + [hbm]
        operands += [*acts, *in_hbm(w_down)]
        scratch += [pltpu.VMEM((local, hidden, wide), BF16), pltpu.SemaphoreType.DMA((1,))]
    return pl.pallas_call(
        functools.partial(up_kernel, part, last, count),
        in_specs=specs,
        out_specs=[vmem] * len(shapes),
        out_shape=shapes,
        scratch_shapes=scratch,
        compiler_params=pltpu.CompilerParams(vmem_limit_bytes=(34 if last else 26) << 20),
        name="expert_up",
    )(*operands)


def down_kernel(tensors, first, tab_ref, *refs):
    acts, (wd_ref, send_ref, keep_ref, wd_buf, sem) = refs[:tensors], refs[tensors:]
    copy = load_down(wd_ref, wd_buf, sem.at[0], first)
    copy.start()
    copy.wait()
    down_product(acts, wd_buf, tab_ref, send_ref, keep_ref)


def expert_down(table, acts, w_down, piece, pieces):
    local, chips, _, rows, hidden = acts[0].shape
    columns = w_down.shape[2] // pieces
    vmem = pl.BlockSpec(memory_space=pltpu.VMEM)
    half = jax.ShapeDtypeStruct((len(acts), chips, rows, columns), BF16)
    return pl.pallas_call(
        functools.partial(down_kernel, len(acts), piece * columns),
        in_specs=[pl.BlockSpec(memory_space=pltpu.SMEM)]
        + [vmem] * len(acts)
        + [pl.BlockSpec(memory_space=pltpu.HBM)],
        out_specs=[vmem] * 2,
        out_shape=[half, half],
        scratch_shapes=[
            pltpu.VMEM((local, hidden, columns), BF16),
            pltpu.SemaphoreType.DMA((1,)),
        ],
        compiler_params=pltpu.CompilerParams(vmem_limit_bytes=20 << 20),
        name="expert_down",
    )(table, *acts, *in_hbm(w_down))


def per_device(
    query,
    latest_key_value,
    cache,
    lengths,
    w_out,
    residual_in,
    norm_gain,
    expert_ids,
    route_weights,
    w_gate,
    w_up,
    w_down,
):
    count = lax.axis_size("expert")
    tensors = lax.axis_size("tensor")
    chips = count // CORES
    me = lax.axis_index("expert")
    mine = lax.axis_index("tensor")
    core = me % CORES
    chip = me // CORES
    token_count = query.shape[0]
    rows = token_count // tensors
    columns = w_out.shape[1]
    local = w_gate.shape[0]
    features = residual_in.shape[1]

    behind = jnp.take(jnp.array(chip_table(chips, -1), jnp.int32), chip, axis=0)
    ahead = jnp.take(jnp.array(chip_table(chips, 1), jnp.int32), chip, axis=0)
    blocks = jnp.concatenate([behind * CORES + core, behind * CORES + (1 - core)])
    table = jnp.concatenate([blocks, me[None], core[None], ahead]).astype(jnp.int32)

    named = expert_ids[:, :, None] == jnp.arange(local * count, dtype=jnp.int32)
    dense = jnp.sum(jnp.where(named, route_weights[:, :, None], 0.0), axis=1)
    high = dense.astype(BF16)
    low = (dense - high.astype(F32)).astype(BF16)
    pair = jnp.stack([high, low], axis=-1).reshape(tensors, rows, count, local * 2)
    pair = jnp.roll(pair, -mine, axis=0)
    pair = pair.transpose(2, 1, 0, 3).reshape(count, rows, tensors * local * 2)
    pair = jnp.pad(pair, ((0, 0), (0, 0), (0, 128 - pair.shape[2])))
    shares = residual_in.reshape(rows, count, columns).transpose(1, 0, 2)
    packed = jnp.concatenate([shares, pair], axis=2)
    given = lax.all_to_all(packed, "expert", split_axis=0, concat_axis=0, tiled=True)
    pair = given[:, :, columns : columns + tensors * local * 2].astype(F32)
    pair = pair.reshape(count, rows, tensors, local, 2).sum(axis=-1)
    weights = pair.transpose(2, 0, 1, 3).reshape(tensors, count * rows, local)

    passed = []
    for j in range(1, tensors + 1):
        part = (mine + j) % tensors
        attended = attend(part, query, latest_key_value, cache, lengths, tensors)
        pieces = chip_gather(attended, chips)
        pieces = pieces + [core_swap(p, chips) for p in pieces]
        adds = [] if j < tensors else passed + [given]
        stream = project(table, pieces, w_out, adds)
        if j < tensors:
            passed.append(tensor_shift(stream, tensors, -j))

    gathered = chip_gather(stream, chips)
    acts = []
    for j in range(tensors):
        held = gathered
        if j:
            held = [tensor_shift(p, tensors, j) for p in gathered]
        held = held + [core_swap(p, chips) for p in held]
        rest = (acts, w_down, 2) if j == tensors - 1 else ()
        act, *more = expert_up(table, j, held, norm_gain, weights, w_gate, w_up, *rest)
        acts.append(act)
        if j == 0:
            mine_rows = more.pop(0)

    half = features // 2
    sums = []
    for part in range(2):
        if part:
            more = expert_down(table, acts, w_down, part, 2)
        send, keep = more
        both = keep.astype(F32) + core_swap(send, chips).astype(F32)
        for axis in (("t", "z") if part == 0 else ("z", "t")):
            if axis == "t":
                kept = both[0]
                for j in range(1, tensors):
                    moved = tensor_shift(both[j].astype(BF16), tensors, -j)
                    kept = kept + moved.astype(F32)
                both = kept[None]
            else:
                both = chip_scatter(lambda s, both=both: both[:, s], chips)[:, None]
        sums.append(both.reshape(rows, half))
    return (mine_rows.astype(F32) + jnp.concatenate(sums, axis=1)).astype(BF16)


def solution(mesh):
    placed = (
        P(("groups", "expert"), "tensor"),
        P(("groups", "expert"), None, "tensor"),
        P(("groups", "expert"), None, None, "tensor"),
        P(("groups", "expert")),
        P("tensor", "expert"),
        P(("groups", "expert", "tensor"), None),
        P(),
        P(("groups", "expert"), None),
        P(("groups", "expert"), None),
        P("expert", None, "tensor"),
        P("expert", None, "tensor"),
        P("expert", "tensor", None),
    )

    return jax.shard_map(
        per_device,
        mesh=mesh,
        in_specs=placed,
        out_specs=P(("groups", "expert", "tensor"), None),
        check_vma=False,
    )
```

time: 454 us -> 133 us (0.29)
  blocking collectives: 156 us -> 0 us
  waiting for transfers between devices: 203 us -> 50.5 us
  Pallas kernels: 0 us -> 33.8 us
  starting transfers between devices: 9.44 us -> 42.9 us
  local copies, waits for them, and re-layouts: 33 us -> 1.34 us
  matrix products: 31.4 us -> 0 us
  between operations: 13.4 us -> 0.35 us
    all_to_all x2 -> x0, blocking collectives: 150 us -> none  [the longest x1 143 us: per_device(): lax.all_to_all(packed, 'expert', split_axis=0, concat_axis=1, tiled=True)]
    all_to_all x2 -> x1, waiting for transfers between devices: 76.5 us -> 0.01 us  [per_device(): lax.all_to_all(packed, 'expert', split_axis=0, concat_axis=0, tiled=True)]
    reduce_scatter x1 -> x0, waiting for transfers between devices: 75.3 us -> none  [per_device(): lax.psum_scatter(partial_out.astype(jnp.bfloat16), 'tensor', scatter_dime...]
    ppermute x0 -> x40, waiting for transfers between devices: none -> 50.5 us  [the longest x15 31.3 us: chip_send(): return lax.ppermute(piece, 'expert', chip_perm(chips, shift))]
    all_gather x1 -> x0, waiting for transfers between devices: 41 us -> none  [per_device(): lax.all_gather(attended, 'expert', axis=0, tiled=True)]
    ppermute x0 -> x40, starting transfers between devices: none -> 39.3 us  [the longest x15 27.1 us: chip_send(): return lax.ppermute(piece, 'expert', chip_perm(chips, shift))]
    pallas_call x0 -> x7, Pallas kernels: none -> 33.8 us  [the longest x2 13.5 us: expert_up(): pl.pallas_call(functools.partial(up_kernel, part, last, count), in_specs=...]
    dot_general x8 -> x0, matrix products: 31.4 us -> none  [the longest x1 12.6 us: per_device(): jnp.einsum('xsf,xfd->xsd', activated, w_down, preferred_element_type=jnp....]
  transfers between devices with their start and end apart: 5 -> 41, of which waited for: 5 -> 16; matrix products, arithmetic and copies ran while one was open for 1% -> 3% of each run, Pallas kernels for 0% -> 11%
where the time goes in v1:
time: 133 us
  waiting for transfers between devices  50.5 us (38%)
  starting transfers between devices  42.9 us (32%)
  Pallas kernels  33.8 us (25%)
  other arithmetic  3.72 us (3%)
  local copies, waits for them, and re-layouts  1.34 us (1%)
    ppermute x15, waiting for transfers between devices, chip_send(): return lax.ppermute(piece, 'expert', chip_perm(chips, shift))  31.3 us
    ppermute x15, starting transfers between devices, chip_send(): return lax.ppermute(piece, 'expert', chip_perm(chips, shift))  27.1 us
    ppermute x7, waiting for transfers between devices, tensor_shift(): lax.ppermute(piece, 'tensor', [((i + shift) % tensors, i) for i in range(...  17.3 us
    pallas_call x2, Pallas kernels, expert_up(): pl.pallas_call(functools.partial(up_kernel, part, last, count), in_specs=...  13.5 us
    pallas_call x2, Pallas kernels, attend(): pl.pallas_call(functools.partial(attention_kernel, chunk, kv_heads, head_...  9.22 us
    ppermute x7, starting transfers between devices, tensor_shift(): lax.ppermute(piece, 'tensor', [((i + shift) % tensors, i) for i in range(...  8.6 us
    pallas_call x2, Pallas kernels, project(): pl.pallas_call(functools.partial(project_kernel, count, steps), in_specs=...  7.22 us
    pallas_call x1, Pallas kernels, expert_down(): pl.pallas_call(functools.partial(down_kernel, len(acts), piece * columns)...  3.86 us
  transfers between devices with their start and end apart: 41, of which 16 were waited for; matrix products, arithmetic and copies ran while one was open for 3% of the time, Pallas kernels for 11%

profile of v1, /device:TPU:0, one launch (start us, length us, event | category | flops | bytes accessed | tf_op | source)
XLA Modules:
  0.0 132.7 jit_solution(12764179039452054924)
XLA Ops:
  0.0 0.7 copy-done
  0.7 4.6 %attend.2.refs_0_ = bf16[24,4096]{1,0:T(8,128)(2,1)S(1)} custom-call(s32[1]{0:T(128)} %bitcast.4.tab_ref, s32[48]{0:T(128)S(1)} %copy-done, bf16[2,24,4096]{2,1,0:T(8,128)(2,1)} %bitcast.96, bf16[2,24,2,256]{3,2,1,0:T(2,128)(2,1)} %bitcast.99, bf16[48,2,128,256]{3,2,1,0:T(8,128)(2,1)} %cache_ref.3), custom_call_target="tpu_custom_call" | custom-call | tf_op jit(solution)/shard_map/attend/pallas_call | solution.py:167
  5.3 3.1 %collective-permute-start.2 = (bf16[24,4096]{1,0:T(8,128)(2,1)S(1)}, bf16[24,4096]{1,0:T(8,128)(2,1)S(1)}, u32[]{:S(2)}, u32[]{:S(2)}) collective-permute-start(bf16[24,4096]{1,0:T(8,128)(2,1)S(1)} %attend.2.refs_0_), channel_id=1, source_target_pairs={{0,4},{2,6},{4,12},{6,14},{8,0},{10,2},{12,8},{14,10},{1,5},{3,7},... | collective-permute-start | bytes 589832 | tf_op jit(solution)/shard_map/ppermute | solution.py:42
  8.4 1.1 collective-permute-start
  9.5 4.6 %attend.3.refs_0_ = bf16[24,4096]{1,0:T(8,128)(2,1)S(1)} custom-call(s32[1]{0:T(128)} %bitcast.7.tab_ref, s32[48]{0:T(128)S(1)} %copy-done.1, bf16[2,24,4096]{2,1,0:T(8,128)(2,1)} %bitcast.97, bf16[2,24,2,256]{3,2,1,0:T(2,128)(2,1)} %bitcast.100, bf16[48,2,128,256]{3,2,1,0:T(8,128)(2,1)} %cache_ref.3), custom_call_target="tpu_custom_call" | custom-call | tf_op jit(solution)/shard_map/attend/pallas_call | solution.py:167
  14.1 1.6 %collective-permute-start.9 = (bf16[24,4096]{1,0:T(8,128)(2,1)S(1)}, bf16[24,4096]{1,0:T(8,128)(2,1)S(1)}, u32[]{:S(2)}, u32[]{:S(2)}) collective-permute-start(bf16[24,4096]{1,0:T(8,128)(2,1)S(1)} %attend.3.refs_0_), channel_id=1, source_target_pairs={{0,4},{2,6},{4,12},{6,14},{8,0},{10,2},{12,8},{14,10},{1,5},{3,7},... | collective-permute-start | bytes 589832 | tf_op jit(solution)/shard_map/ppermute | solution.py:42
  15.7 1.4 %collective-permute-start.7 = (bf16[24,4096]{1,0:T(8,128)(2,1)S(1)}, bf16[24,4096]{1,0:T(8,128)(2,1)S(1)}, u32[]{:S(2)}, u32[]{:S(2)}) collective-permute-start(bf16[24,4096]{1,0:T(8,128)(2,1)S(1)} %attend.3.refs_0_), channel_id=1, source_target_pairs={{0,8},{2,10},{4,0},{6,2},{8,12},{10,14},{12,4},{14,6},{1,9},{3,11}... | collective-permute-start | bytes 589832 | tf_op jit(solution)/shard_map/ppermute | solution.py:42
  17.2 9.7 %collective-permute-done.7.refs_1_ = bf16[24,4096]{1,0:T(8,128)(2,1)S(1)} collective-permute-done((bf16[24,4096]{1,0:T(8,128)(2,1)S(1)}, bf16[24,4096]{1,0:T(8,128)(2,1)S(1)}, u32[]{:S(2)}, u32[]{:S(2)}) %collective-permute-start.7) | collective-permute-done | bytes 196640 | tf_op jit(solution)/shard_map/ppermute | solution.py:42
  26.9 1.8 %collective-permute-start.8 = (bf16[24,4096]{1,0:T(8,128)(2,1)S(1)}, bf16[24,4096]{1,0:T(8,128)(2,1)S(1)}, u32[]{:S(2)}, u32[]{:S(2)}) collective-permute-start(bf16[24,4096]{1,0:T(8,128)(2,1)S(1)} %collective-permute-done.7.refs_1_), channel_id=1, source_target_pairs={{0,8},{2,10},{4,0},{6,2},{8,12},{10,14},{12,4},{14,6},{1,9},{3,11}... | collective-permute-start | bytes 589832 | tf_op jit(solution)/shard_map/ppermute | solution.py:42
  28.9 0.7 fusion.9
  29.7 3.7 %all-to-all-start = ((bf16[8,24,640]{2,1,0:T(8,128)(2,1)}), bf16[8,24,640]{2,1,0:T(8,128)(2,1)S(1)}, u32[]{:S(2)}, u32[]{:S(2)}) async-start(bf16[8,24,640]{2,1,0:T(8,128)(2,1)} %fusion.9), calls=%async_computation | async-start | bytes 491520 | tf_op jit(solution)/shard_map/all_to_all | solution.py:462
  33.9 2.9 %collective-permute-start.1 = (bf16[24,4096]{1,0:T(8,128)(2,1)S(1)}, bf16[24,4096]{1,0:T(8,128)(2,1)S(1)}, u32[]{:S(2)}, u32[]{:S(2)}) collective-permute-start(bf16[24,4096]{1,0:T(8,128)(2,1)S(1)} %collective-permute-done.refs_1_), channel_id=1, source_target_pairs={{0,8},{2,10},{4,0},{6,2},{8,12},{10,14},{12,4},{14,6},{1,9},{3,11}... | collective-permute-start | bytes 589832 | tf_op jit(solution)/shard_map/ppermute | solution.py:42
  37.3 0.7 fusion.21
  38.0 0.7 broadcast_add_fusion
  38.8 5.4 %collective-permute-done.1.refs_2_ = bf16[24,4096]{1,0:T(8,128)(2,1)S(1)} collective-permute-done((bf16[24,4096]{1,0:T(8,128)(2,1)S(1)}, bf16[24,4096]{1,0:T(8,128)(2,1)S(1)}, u32[]{:S(2)}, u32[]{:S(2)}) %collective-permute-start.1) | collective-permute-done | bytes 196640 | tf_op jit(solution)/shard_map/ppermute | solution.py:42
  44.9 3.9 %project.2 = bf16[8,24,512]{2,1,0:T(8,128)(2,1)} custom-call(s32[14]{0:T(128)S(1)} %concatenate.13.tab_ref, bf16[24,4096]{1,0:T(8,128)(2,1)S(1)} %attend.3.refs_0_, bf16[24,4096]{1,0:T(8,128)(2,1)S(1)} %collective-permute-done.7.refs_1_, bf16[24,4096]{1,0:T(8,128)(2,1)S(1)} %collective-permute-done.8.refs_2_, ...), custom_call_target="tpu_custom_call" | custom-call | tf_op jit(solution)/shard_map/project/pallas_call | solution.py:243
  48.8 1.6 %collective-permute-start.14 = (bf16[8,24,512]{2,1,0:T(8,128)(2,1)}, bf16[8,24,512]{2,1,0:T(8,128)(2,1)S(1)}, u32[]{:S(2)}, u32[]{:S(2)}) collective-permute-start(bf16[8,24,512]{2,1,0:T(8,128)(2,1)} %project.2), channel_id=1, source_target_pairs={{1,0},{0,1},{3,2},{2,3},{5,4},{4,5},{7,6},{6,7},{9,8},{8,9},{11,10... | collective-permute-start | bytes 589832 | tf_op jit(solution)/shard_map/ppermute | solution.py:50
  50.4 5.9 %collective-permute-done.14.refs_9_ = bf16[8,24,512]{2,1,0:T(8,128)(2,1)S(1)} collective-permute-done((bf16[8,24,512]{2,1,0:T(8,128)(2,1)}, bf16[8,24,512]{2,1,0:T(8,128)(2,1)S(1)}, u32[]{:S(2)}, u32[]{:S(2)}) %collective-permute-start.14) | collective-permute-done | bytes 196640 | tf_op jit(solution)/shard_map/ppermute | solution.py:50
  56.4 3.3 %project.3.refs_0_ = bf16[8,24,512]{2,1,0:T(8,128)(2,1)S(1)} custom-call(s32[14]{0:T(128)S(1)} %concatenate.13.tab_ref, bf16[24,4096]{1,0:T(8,128)(2,1)S(1)} %attend.2.refs_0_, bf16[24,4096]{1,0:T(8,128)(2,1)S(1)} %collective-permute-done.refs_1_, bf16[24,4096]{1,0:T(8,128)(2,1)S(1)} %collective-permute-done.1.refs_2_, ...), custom_call_target="tpu_custom_call" | custom-call | tf_op jit(solution)/shard_map/project/pallas_call | solution.py:243
  59.6 1.8 %collective-permute-start.15 = (bf16[8,24,512]{2,1,0:T(8,128)(2,1)S(1)}, bf16[8,24,512]{2,1,0:T(8,128)(2,1)S(1)}, u32[]{:S(2)}, u32[]{:S(2)}) collective-permute-start(bf16[8,24,512]{2,1,0:T(8,128)(2,1)S(1)} %project.3.refs_0_), channel_id=1, source_target_pairs={{0,8},{2,10},{4,0},{6,2},{8,12},{10,14},{12,4},{14,6},{1,9},{3,11}... | collective-permute-start | bytes 589832 | tf_op jit(solution)/shard_map/ppermute | solution.py:42
  61.4 1.1 collective-permute-start.17
  62.5 1.5 %collective-permute-start.22 = (bf16[8,24,512]{2,1,0:T(8,128)(2,1)S(1)}, bf16[8,24,512]{2,1,0:T(8,128)(2,1)S(1)}, u32[]{:S(2)}, u32[]{:S(2)}) collective-permute-start(bf16[8,24,512]{2,1,0:T(8,128)(2,1)S(1)} %project.3.refs_0_), channel_id=1, source_target_pairs={{1,0},{0,1},{3,2},{2,3},{5,4},{4,5},{7,6},{6,7},{9,8},{8,9},{11,10... | collective-permute-start | bytes 589832 | tf_op jit(solution)/shard_map/ppermute | solution.py:50
  64.0 4.0 %collective-permute-done.15.refs_1_ = bf16[8,24,512]{2,1,0:T(8,128)(2,1)S(1)} collective-permute-done((bf16[8,24,512]{2,1,0:T(8,128)(2,1)S(1)}, bf16[8,24,512]{2,1,0:T(8,128)(2,1)S(1)}, u32[]{:S(2)}, u32[]{:S(2)}) %collective-permute-start.15) | collective-permute-done | bytes 196640 | tf_op jit(solution)/shard_map/ppermute | solution.py:42
  68.0 2.1 %collective-permute-start.16 = (bf16[8,24,512]{2,1,0:T(8,128)(2,1)S(1)}, bf16[8,24,512]{2,1,0:T(8,128)(2,1)S(1)}, u32[]{:S(2)}, u32[]{:S(2)}) collective-permute-start(bf16[8,24,512]{2,1,0:T(8,128)(2,1)S(1)} %collective-permute-done.15.refs_1_), channel_id=1, source_target_pairs={{0,8},{2,10},{4,0},{6,2},{8,12},{10,14},{12,4},{14,6},{1,9},{3,11}... | collective-permute-start | bytes 589832 | tf_op jit(solution)/shard_map/ppermute | solution.py:42
  70.1 3.1 %collective-permute-done.17.refs_3_ = bf16[8,24,512]{2,1,0:T(8,128)(2,1)S(1)} collective-permute-done((bf16[8,24,512]{2,1,0:T(8,128)(2,1)S(1)}, bf16[8,24,512]{2,1,0:T(8,128)(2,1)S(1)}, u32[]{:S(2)}, u32[]{:S(2)}) %collective-permute-start.17) | collective-permute-done | bytes 196640 | tf_op jit(solution)/shard_map/ppermute | solution.py:42
  73.2 1.5 %collective-permute-start.25 = (bf16[8,24,512]{2,1,0:T(8,128)(2,1)S(1)}, bf16[8,24,512]{2,1,0:T(8,128)(2,1)S(1)}, u32[]{:S(2)}, u32[]{:S(2)}) collective-permute-start(bf16[8,24,512]{2,1,0:T(8,128)(2,1)S(1)} %collective-permute-done.17.refs_3_), channel_id=1, source_target_pairs={{1,0},{0,1},{3,2},{2,3},{5,4},{4,5},{7,6},{6,7},{9,8},{8,9},{11,10... | collective-permute-start | bytes 589832 | tf_op jit(solution)/shard_map/ppermute | solution.py:50
  75.4 0.9 collective-permute-done.16.refs_2_
  76.3 1.5 %collective-permute-start.24 = (bf16[8,24,512]{2,1,0:T(8,128)(2,1)S(1)}, bf16[8,24,512]{2,1,0:T(8,128)(2,1)S(1)}, u32[]{:S(2)}, u32[]{:S(2)}) collective-permute-start(bf16[8,24,512]{2,1,0:T(8,128)(2,1)S(1)} %collective-permute-done.16.refs_2_), channel_id=1, source_target_pairs={{1,0},{0,1},{3,2},{2,3},{5,4},{4,5},{7,6},{6,7},{9,8},{8,9},{11,10... | collective-permute-start | bytes 589832 | tf_op jit(solution)/shard_map/ppermute | solution.py:50
  77.8 2.1 %collective-permute-done.25.refs_3_ = bf16[8,24,512]{2,1,0:T(8,128)(2,1)S(1)} collective-permute-done((bf16[8,24,512]{2,1,0:T(8,128)(2,1)S(1)}, bf16[8,24,512]{2,1,0:T(8,128)(2,1)S(1)}, u32[]{:S(2)}, u32[]{:S(2)}) %collective-permute-start.25) | collective-permute-done | bytes 196640 | tf_op jit(solution)/shard_map/ppermute | solution.py:50
  80.5 3.7 %collective-permute-done.23.refs_1_ = bf16[8,24,512]{2,1,0:T(8,128)(2,1)S(1)} collective-permute-done((bf16[8,24,512]{2,1,0:T(8,128)(2,1)S(1)}, bf16[8,24,512]{2,1,0:T(8,128)(2,1)S(1)}, u32[]{:S(2)}, u32[]{:S(2)}) %collective-permute-start.23) | collective-permute-done | bytes 196640 | tf_op jit(solution)/shard_map/ppermute | solution.py:50
  84.7 2.6 %collective-permute-done.24.refs_2_ = bf16[8,24,512]{2,1,0:T(8,128)(2,1)S(1)} collective-permute-done((bf16[8,24,512]{2,1,0:T(8,128)(2,1)S(1)}, bf16[8,24,512]{2,1,0:T(8,128)(2,1)S(1)}, u32[]{:S(2)}, u32[]{:S(2)}) %collective-permute-start.24) | collective-permute-done | bytes 196640 | tf_op jit(solution)/shard_map/ppermute | solution.py:50
  87.6 5.8 %expert_up.2 = (bf16[2,4,2,24,384]{4,3,2,1,0:T(8,128)(2,1)S(1)}, bf16[24,4096]{1,0:T(8,128)(2,1)S(1)}) custom-call(s32[14]{0:T(128)S(1)} %concatenate.13.tab_ref, bf16[8,24,512]{2,1,0:T(8,128)(2,1)S(1)} %project.3.refs_0_, bf16[8,24,512]{2,1,0:T(8,128)(2,1)S(1)} %collective-permute-done.15.refs_1_, bf16[8,24,512]{2,1,0:T(8,128)(2,1)S(1)} %collective-permute-done.16.refs_2_, ...), custom_call_target="tpu_custom_call" | custom-call | tf_op jit(solution)/shard_map/expert_up/pallas_call | solution.py:380
  93.4 7.7 %expert_up.3 = (bf16[2,4,2,24,384]{4,3,2,1,0:T(8,128)(2,1)S(1)}, bf16[2,4,24,2048]{3,2,1,0:T(8,128)(2,1)S(1)}, bf16[2,4,24,2048]{3,2,1,0:T(8,128)(2,1)S(1)}) custom-call(s32[14]{0:T(128)S(1)} %concatenate.13.tab_ref, bf16[8,24,512]{2,1,0:T(8,128)(2,1)S(1)} %collective-permute-done.22.refs_0_, bf16[8,24,512]{2,1,0:T(8,128)(2,1)S(1)} %collective-permute-done.23.refs_1_, ...), custom_call_target="tpu_custom_call" | custom-call | tf_op jit(solution)/shard_map/expert_up/pallas_call | solution.py:380
  101.2 3.9 %expert_down.1 = (bf16[2,4,24,2048]{3,2,1,0:T(8,128)(2,1)S(1)}, bf16[2,4,24,2048]{3,2,1,0:T(8,128)(2,1)S(1)}) custom-call(s32[14]{0:T(128)S(1)} %concatenate.13.tab_ref, bf16[2,4,2,24,384]{4,3,2,1,0:T(8,128)(2,1)S(1)} %get-tuple-element.14.refs_12_.refs_0_, bf16[2,4,2,24,384]{4,3,2,1,0:T(8,128)(2,1)S(1)} %get-tuple-element.17.refs_1_, ...), custom_call_target="tpu_custom_call" | custom-call | tf_op jit(solution)/shard_map/expert_down/pallas_call | solution.py:404
  105.1 0.5 collective-permute-start.35
  105.7 1.8 %collective-permute-done.35 = bf16[2,4,24,2048]{3,2,1,0:T(8,128)(2,1)S(1)} collective-permute-done((bf16[2,4,24,2048]{3,2,1,0:T(8,128)(2,1)S(1)}, bf16[2,4,24,2048]{3,2,1,0:T(8,128)(2,1)S(1)}, u32[]{:S(2)}, u32[]{:S(2)}) %collective-permute-start.35) | collective-permute-done | bytes 786464 | tf_op jit(solution)/shard_map/ppermute | solution.py:46
  107.8 2.2 %collective-permute-start.36 = (bf16[2,24,2048]{2,1,0:T(8,128)(2,1)S(1)}, bf16[2,24,2048]{2,1,0:T(8,128)(2,1)S(1)}, u32[]{:S(2)}, u32[]{:S(2)}) collective-permute-start(bf16[2,24,2048]{2,1,0:T(8,128)(2,1)S(1)} %get-tuple-element.37), channel_id=1, source_target_pairs={{0,8},{2,10},{4,0},{6,2},{8,12},{10,14},{12,4},{14,6},{1,9},{3,11}... | collective-permute-start | bytes 589832 | tf_op jit(solution)/shard_map/ppermute | solution.py:42
  110.3 1.6 %collective-permute-start.31 = (bf16[4,24,2048]{2,1,0:T(8,128)(2,1)S(1)}, bf16[4,24,2048]{2,1,0:T(8,128)(2,1)S(1)}, u32[]{:S(2)}, u32[]{:S(2)}) collective-permute-start(bf16[4,24,2048]{2,1,0:T(8,128)(2,1)S(1)} %fusion.3), channel_id=1, source_target_pairs={{1,0},{0,1},{3,2},{2,3},{5,4},{4,5},{7,6},{6,7},{9,8},{8,9},{11,10... | collective-permute-start | bytes 1179656 | tf_op jit(solution)/shard_map/ppermute | solution.py:50
  111.9 3.5 %collective-permute-done.36 = bf16[2,24,2048]{2,1,0:T(8,128)(2,1)S(1)} collective-permute-done((bf16[2,24,2048]{2,1,0:T(8,128)(2,1)S(1)}, bf16[2,24,2048]{2,1,0:T(8,128)(2,1)S(1)}, u32[]{:S(2)}, u32[]{:S(2)}) %collective-permute-start.36) | collective-permute-done | bytes 196640 | tf_op jit(solution)/shard_map/ppermute | solution.py:42
  115.4 3.4 %collective-permute-start.37 = (bf16[2,24,2048]{2,1,0:T(8,128)(2,1)S(1)}, bf16[2,24,2048]{2,1,0:T(8,128)(2,1)S(1)}, u32[]{:S(2)}, u32[]{:S(2)}) collective-permute-start(bf16[2,24,2048]{2,1,0:T(8,128)(2,1)S(1)} %fusion.5), channel_id=1, source_target_pairs={{0,8},{2,10},{4,0},{6,2},{8,12},{10,14},{12,4},{14,6},{1,9},{3,11}... | collective-permute-start | bytes 589832 | tf_op jit(solution)/shard_map/ppermute | solution.py:42
  118.9 2.6 %collective-permute-done.31 = bf16[4,24,2048]{2,1,0:T(8,128)(2,1)S(1)} collective-permute-done((bf16[4,24,2048]{2,1,0:T(8,128)(2,1)S(1)}, bf16[4,24,2048]{2,1,0:T(8,128)(2,1)S(1)}, u32[]{:S(2)}, u32[]{:S(2)}) %collective-permute-start.31) | collective-permute-done | bytes 393248 | tf_op jit(solution)/shard_map/ppermute | solution.py:50
  121.6 1.1 collective-permute-start.32
  122.7 1.0 collective-permute-start.34
  123.7 1.5 %collective-permute-done.38 = bf16[2,24,2048]{2,1,0:T(8,128)(2,1)S(1)} collective-permute-done((bf16[2,24,2048]{2,1,0:T(8,128)(2,1)S(1)}, bf16[2,24,2048]{2,1,0:T(8,128)(2,1)S(1)}, u32[]{:S(2)}, u32[]{:S(2)}) %collective-permute-start.38) | collective-permute-done | bytes 196640 | tf_op jit(solution)/shard_map/ppermute | solution.py:42
  125.8 1.3 collective-permute-done.32
  127.1 2.6 %collective-permute-start.33 = (bf16[1,24,2048]{2,1,0:T(8,128)(2,1)S(1)}, bf16[1,24,2048]{2,1,0:T(8,128)(2,1)S(1)}, u32[]{:S(2)}, u32[]{:S(2)}) collective-permute-start(bf16[1,24,2048]{2,1,0:T(8,128)(2,1)S(1)} %fusion.12), channel_id=1, source_target_pairs={{0,8},{2,10},{4,0},{6,2},{8,12},{10,14},{12,4},{14,6},{1,9},{3,11}... | collective-permute-start | bytes 294920 | tf_op jit(solution)/shard_map/ppermute | solution.py:42
  130.0 1.9 %collective-permute-done.33 = bf16[1,24,2048]{2,1,0:T(8,128)(2,1)S(1)} collective-permute-done((bf16[1,24,2048]{2,1,0:T(8,128)(2,1)S(1)}, bf16[1,24,2048]{2,1,0:T(8,128)(2,1)S(1)}, u32[]{:S(2)}, u32[]{:S(2)}) %collective-permute-start.33) | collective-permute-done | bytes 98336 | tf_op jit(solution)/shard_map/ppermute | solution.py:42
  132.0 0.7 fusion.8
  (84 shorter events, 6.0 us)
Async XLA Ops:
  0.0 0.7 copy-start
  0.7 8.8 %copy-start.1 = (s32[48]{0:T(128)S(1)}, s32[48]{0:T(128)}, u32[]{:S(2)}) copy-start(s32[48]{0:T(128)} %len_ref.3) | copy-start | bytes 580
  5.3 28.6 %collective-permute-start.2 = (bf16[24,4096]{1,0:T(8,128)(2,1)S(1)}, bf16[24,4096]{1,0:T(8,128)(2,1)S(1)}, u32[]{:S(2)}, u32[]{:S(2)}) collective-permute-start(bf16[24,4096]{1,0:T(8,128)(2,1)S(1)} %attend.2.refs_0_), channel_id=1, source_target_pairs={{0,4},{2,6},{4,12},{6,14},{8,0},{10,2},{12,8},{14,10},{1,5},{3,7},... | collective-permute-start | bytes 589832 | tf_op jit(solution)/shard_map/ppermute | solution.py:42
  8.4 25.5 %collective-permute-start = (bf16[24,4096]{1,0:T(8,128)(2,1)S(1)}, bf16[24,4096]{1,0:T(8,128)(2,1)S(1)}, u32[]{:S(2)}, u32[]{:S(2)}) collective-permute-start(bf16[24,4096]{1,0:T(8,128)(2,1)S(1)} %attend.2.refs_0_), channel_id=1, source_target_pairs={{0,8},{2,10},{4,0},{6,2},{8,12},{10,14},{12,4},{14,6},{1,9},{3,11}... | collective-permute-start | bytes 589832 | tf_op jit(solution)/shard_map/ppermute | solution.py:42
  9.5 7.6 %copy-start.4 = (f32[48,8]{0,1:T(8,128)S(1)}, f32[48,8]{0,1:T(8,128)}, u32[]{:S(2)}) copy-start(f32[48,8]{0,1:T(8,128)} %param.24) | copy-start | bytes 4612
  9.5 7.6 %copy-start.5 = (s32[48,8]{0,1:T(8,128)S(1)}, s32[48,8]{0,1:T(8,128)}, u32[]{:S(2)}) copy-start(s32[48,8]{0,1:T(8,128)} %param.23) | copy-start | bytes 4612
  9.5 19.5 %copy-start.2 = (bf16[24,4096]{1,0:T(8,128)(2,1)S(1)}, bf16[24,4096]{1,0:T(8,128)(2,1)}, u32[]{:S(2)}) copy-start(bf16[24,4096]{1,0:T(8,128)(2,1)} %param.21) | copy-start | bytes 589828
  14.1 22.7 %collective-permute-start.9 = (bf16[24,4096]{1,0:T(8,128)(2,1)S(1)}, bf16[24,4096]{1,0:T(8,128)(2,1)S(1)}, u32[]{:S(2)}, u32[]{:S(2)}) collective-permute-start(bf16[24,4096]{1,0:T(8,128)(2,1)S(1)} %attend.3.refs_0_), channel_id=1, source_target_pairs={{0,4},{2,6},{4,12},{6,14},{8,0},{10,2},{12,8},{14,10},{1,5},{3,7},... | collective-permute-start | bytes 589832 | tf_op jit(solution)/shard_map/ppermute | solution.py:42
  15.7 11.3 %collective-permute-start.7 = (bf16[24,4096]{1,0:T(8,128)(2,1)S(1)}, bf16[24,4096]{1,0:T(8,128)(2,1)S(1)}, u32[]{:S(2)}, u32[]{:S(2)}) collective-permute-start(bf16[24,4096]{1,0:T(8,128)(2,1)S(1)} %attend.3.refs_0_), channel_id=1, source_target_pairs={{0,8},{2,10},{4,0},{6,2},{8,12},{10,14},{12,4},{14,6},{1,9},{3,11}... | collective-permute-start | bytes 589832 | tf_op jit(solution)/shard_map/ppermute | solution.py:42
  26.9 9.8 %collective-permute-start.8 = (bf16[24,4096]{1,0:T(8,128)(2,1)S(1)}, bf16[24,4096]{1,0:T(8,128)(2,1)S(1)}, u32[]{:S(2)}, u32[]{:S(2)}) collective-permute-start(bf16[24,4096]{1,0:T(8,128)(2,1)S(1)} %collective-permute-done.7.refs_1_), channel_id=1, source_target_pairs={{0,8},{2,10},{4,0},{6,2},{8,12},{10,14},{12,4},{14,6},{1,9},{3,11}... | collective-permute-start | bytes 589832 | tf_op jit(solution)/shard_map/ppermute | solution.py:42
  29.7 20.7 %all-to-all-start = ((bf16[8,24,640]{2,1,0:T(8,128)(2,1)}), bf16[8,24,640]{2,1,0:T(8,128)(2,1)S(1)}, u32[]{:S(2)}, u32[]{:S(2)}) async-start(bf16[8,24,640]{2,1,0:T(8,128)(2,1)} %fusion.9), calls=%async_computation | async-start | bytes 491520 | tf_op jit(solution)/shard_map/all_to_all | solution.py:462
  33.3 5.4 %collective-permute-start.10 = (bf16[24,4096]{1,0:T(8,128)(2,1)S(1)}, bf16[24,4096]{1,0:T(8,128)(2,1)S(1)}, u32[]{:S(2)}, u32[]{:S(2)}) collective-permute-start(bf16[24,4096]{1,0:T(8,128)(2,1)S(1)} %attend.3.refs_0_), channel_id=1, source_target_pairs={{0,2},{2,0},{4,6},{6,4},{8,10},{10,8},{12,14},{14,12},{1,3},{3,1},... | collective-permute-start | bytes 589832 | tf_op jit(solution)/shard_map/ppermute | solution.py:46
  33.8 11.0 %collective-permute-start.11 = (bf16[24,4096]{1,0:T(8,128)(2,1)S(1)}, bf16[24,4096]{1,0:T(8,128)(2,1)S(1)}, u32[]{:S(2)}, u32[]{:S(2)}) collective-permute-start(bf16[24,4096]{1,0:T(8,128)(2,1)S(1)} %collective-permute-done.7.refs_1_), channel_id=1, source_target_pairs={{0,2},{2,0},{4,6},{6,4},{8,10},{10,8},{12,14},{14,12},{1,3},{3,1},... | collective-permute-start | bytes 589832 | tf_op jit(solution)/shard_map/ppermute | solution.py:46
  33.9 10.4 %collective-permute-start.1 = (bf16[24,4096]{1,0:T(8,128)(2,1)S(1)}, bf16[24,4096]{1,0:T(8,128)(2,1)S(1)}, u32[]{:S(2)}, u32[]{:S(2)}) collective-permute-start(bf16[24,4096]{1,0:T(8,128)(2,1)S(1)} %collective-permute-done.refs_1_), channel_id=1, source_target_pairs={{0,8},{2,10},{4,0},{6,2},{8,12},{10,14},{12,4},{14,6},{1,9},{3,11}... | collective-permute-start | bytes 589832 | tf_op jit(solution)/shard_map/ppermute | solution.py:42
  36.8 7.5 %collective-permute-start.13 = (bf16[24,4096]{1,0:T(8,128)(2,1)S(1)}, bf16[24,4096]{1,0:T(8,128)(2,1)S(1)}, u32[]{:S(2)}, u32[]{:S(2)}) collective-permute-start(bf16[24,4096]{1,0:T(8,128)(2,1)S(1)} %collective-permute-done.9.refs_3_), channel_id=1, source_target_pairs={{0,2},{2,0},{4,6},{6,4},{8,10},{10,8},{12,14},{14,12},{1,3},{3,1},... | collective-permute-start | bytes 589832 | tf_op jit(solution)/shard_map/ppermute | solution.py:46
  36.8 8.1 %collective-permute-start.12 = (bf16[24,4096]{1,0:T(8,128)(2,1)S(1)}, bf16[24,4096]{1,0:T(8,128)(2,1)S(1)}, u32[]{:S(2)}, u32[]{:S(2)}) collective-permute-start(bf16[24,4096]{1,0:T(8,128)(2,1)S(1)} %collective-permute-done.8.refs_2_), channel_id=1, source_target_pairs={{0,2},{2,0},{4,6},{6,4},{8,10},{10,8},{12,14},{14,12},{1,3},{3,1},... | collective-permute-start | bytes 589832 | tf_op jit(solution)/shard_map/ppermute | solution.py:46
  38.7 11.6 %collective-permute-start.3 = (bf16[24,4096]{1,0:T(8,128)(2,1)S(1)}, bf16[24,4096]{1,0:T(8,128)(2,1)S(1)}, u32[]{:S(2)}, u32[]{:S(2)}) collective-permute-start(bf16[24,4096]{1,0:T(8,128)(2,1)S(1)} %attend.2.refs_0_), channel_id=1, source_target_pairs={{0,2},{2,0},{4,6},{6,4},{8,10},{10,8},{12,14},{14,12},{1,3},{3,1},... | collective-permute-start | bytes 589832 | tf_op jit(solution)/shard_map/ppermute | solution.py:46
  44.3 6.1 %collective-permute-start.4 = (bf16[24,4096]{1,0:T(8,128)(2,1)S(1)}, bf16[24,4096]{1,0:T(8,128)(2,1)S(1)}, u32[]{:S(2)}, u32[]{:S(2)}) collective-permute-start(bf16[24,4096]{1,0:T(8,128)(2,1)S(1)} %collective-permute-done.refs_1_), channel_id=1, source_target_pairs={{0,2},{2,0},{4,6},{6,4},{8,10},{10,8},{12,14},{14,12},{1,3},{3,1},... | collective-permute-start | bytes 589832 | tf_op jit(solution)/shard_map/ppermute | solution.py:46
  44.3 6.1 %collective-permute-start.6 = (bf16[24,4096]{1,0:T(8,128)(2,1)S(1)}, bf16[24,4096]{1,0:T(8,128)(2,1)S(1)}, u32[]{:S(2)}, u32[]{:S(2)}) collective-permute-start(bf16[24,4096]{1,0:T(8,128)(2,1)S(1)} %collective-permute-done.2.refs_3_), channel_id=1, source_target_pairs={{0,2},{2,0},{4,6},{6,4},{8,10},{10,8},{12,14},{14,12},{1,3},{3,1},... | collective-permute-start | bytes 589832 | tf_op jit(solution)/shard_map/ppermute | solution.py:46
  44.8 5.6 %collective-permute-start.5 = (bf16[24,4096]{1,0:T(8,128)(2,1)S(1)}, bf16[24,4096]{1,0:T(8,128)(2,1)S(1)}, u32[]{:S(2)}, u32[]{:S(2)}) collective-permute-start(bf16[24,4096]{1,0:T(8,128)(2,1)S(1)} %collective-permute-done.1.refs_2_), channel_id=1, source_target_pairs={{0,2},{2,0},{4,6},{6,4},{8,10},{10,8},{12,14},{14,12},{1,3},{3,1},... | collective-permute-start | bytes 589832 | tf_op jit(solution)/shard_map/ppermute | solution.py:46
  48.8 29.0 %copy-start.3 = (bf16[4096]{0:T(1024)(128)(2,1)S(1)}, bf16[4096]{0:T(1024)(128)(2,1)}, u32[]{:S(2)}) copy-start(bf16[4096]{0:T(1024)(128)(2,1)} %param.22) | copy-start | bytes 24580
  48.8 7.5 %collective-permute-start.14 = (bf16[8,24,512]{2,1,0:T(8,128)(2,1)}, bf16[8,24,512]{2,1,0:T(8,128)(2,1)S(1)}, u32[]{:S(2)}, u32[]{:S(2)}) collective-permute-start(bf16[8,24,512]{2,1,0:T(8,128)(2,1)} %project.2), channel_id=1, source_target_pairs={{1,0},{0,1},{3,2},{2,3},{5,4},{4,5},{7,6},{6,7},{9,8},{8,9},{11,10... | collective-permute-start | bytes 589832 | tf_op jit(solution)/shard_map/ppermute | solution.py:50
  59.6 8.4 %collective-permute-start.15 = (bf16[8,24,512]{2,1,0:T(8,128)(2,1)S(1)}, bf16[8,24,512]{2,1,0:T(8,128)(2,1)S(1)}, u32[]{:S(2)}, u32[]{:S(2)}) collective-permute-start(bf16[8,24,512]{2,1,0:T(8,128)(2,1)S(1)} %project.3.refs_0_), channel_id=1, source_target_pairs={{0,8},{2,10},{4,0},{6,2},{8,12},{10,14},{12,4},{14,6},{1,9},{3,11}... | collective-permute-start | bytes 589832 | tf_op jit(solution)/shard_map/ppermute | solution.py:42
  61.4 11.8 %collective-permute-start.17 = (bf16[8,24,512]{2,1,0:T(8,128)(2,1)S(1)}, bf16[8,24,512]{2,1,0:T(8,128)(2,1)S(1)}, u32[]{:S(2)}, u32[]{:S(2)}) collective-permute-start(bf16[8,24,512]{2,1,0:T(8,128)(2,1)S(1)} %project.3.refs_0_), channel_id=1, source_target_pairs={{0,4},{2,6},{4,12},{6,14},{8,0},{10,2},{12,8},{14,10},{1,5},{3,7},... | collective-permute-start | bytes 589832 | tf_op jit(solution)/shard_map/ppermute | solution.py:42
  62.5 12.2 %collective-permute-start.22 = (bf16[8,24,512]{2,1,0:T(8,128)(2,1)S(1)}, bf16[8,24,512]{2,1,0:T(8,128)(2,1)S(1)}, u32[]{:S(2)}, u32[]{:S(2)}) collective-permute-start(bf16[8,24,512]{2,1,0:T(8,128)(2,1)S(1)} %project.3.refs_0_), channel_id=1, source_target_pairs={{1,0},{0,1},{3,2},{2,3},{5,4},{4,5},{7,6},{6,7},{9,8},{8,9},{11,10... | collective-permute-start | bytes 589832 | tf_op jit(solution)/shard_map/ppermute | solution.py:50
  64.0 11.2 %collective-permute-start.18 = (bf16[8,24,512]{2,1,0:T(8,128)(2,1)S(1)}, bf16[8,24,512]{2,1,0:T(8,128)(2,1)S(1)}, u32[]{:S(2)}, u32[]{:S(2)}) collective-permute-start(bf16[8,24,512]{2,1,0:T(8,128)(2,1)S(1)} %project.3.refs_0_), channel_id=1, source_target_pairs={{0,2},{2,0},{4,6},{6,4},{8,10},{10,8},{12,14},{14,12},{1,3},{3,1},... | collective-permute-start | bytes 589832 | tf_op jit(solution)/shard_map/ppermute | solution.py:46
  68.0 8.3 %collective-permute-start.16 = (bf16[8,24,512]{2,1,0:T(8,128)(2,1)S(1)}, bf16[8,24,512]{2,1,0:T(8,128)(2,1)S(1)}, u32[]{:S(2)}, u32[]{:S(2)}) collective-permute-start(bf16[8,24,512]{2,1,0:T(8,128)(2,1)S(1)} %collective-permute-done.15.refs_1_), channel_id=1, source_target_pairs={{0,8},{2,10},{4,0},{6,2},{8,12},{10,14},{12,4},{14,6},{1,9},{3,11}... | collective-permute-start | bytes 589832 | tf_op jit(solution)/shard_map/ppermute | solution.py:42
  73.2 6.8 %collective-permute-start.25 = (bf16[8,24,512]{2,1,0:T(8,128)(2,1)S(1)}, bf16[8,24,512]{2,1,0:T(8,128)(2,1)S(1)}, u32[]{:S(2)}, u32[]{:S(2)}) collective-permute-start(bf16[8,24,512]{2,1,0:T(8,128)(2,1)S(1)} %collective-permute-done.17.refs_3_), channel_id=1, source_target_pairs={{1,0},{0,1},{3,2},{2,3},{5,4},{4,5},{7,6},{6,7},{9,8},{8,9},{11,10... | collective-permute-start | bytes 589832 | tf_op jit(solution)/shard_map/ppermute | solution.py:50
  74.7 5.3 %collective-permute-start.21 = (bf16[8,24,512]{2,1,0:T(8,128)(2,1)S(1)}, bf16[8,24,512]{2,1,0:T(8,128)(2,1)S(1)}, u32[]{:S(2)}, u32[]{:S(2)}) collective-permute-start(bf16[8,24,512]{2,1,0:T(8,128)(2,1)S(1)} %collective-permute-done.17.refs_3_), channel_id=1, source_target_pairs={{0,2},{2,0},{4,6},{6,4},{8,10},{10,8},{12,14},{14,12},{1,3},{3,1},... | collective-permute-start | bytes 589832 | tf_op jit(solution)/shard_map/ppermute | solution.py:46
  74.7 9.5 %collective-permute-start.23 = (bf16[8,24,512]{2,1,0:T(8,128)(2,1)S(1)}, bf16[8,24,512]{2,1,0:T(8,128)(2,1)S(1)}, u32[]{:S(2)}, u32[]{:S(2)}) collective-permute-start(bf16[8,24,512]{2,1,0:T(8,128)(2,1)S(1)} %collective-permute-done.15.refs_1_), channel_id=1, source_target_pairs={{1,0},{0,1},{3,2},{2,3},{5,4},{4,5},{7,6},{6,7},{9,8},{8,9},{11,10... | collective-permute-start | bytes 589832 | tf_op jit(solution)/shard_map/ppermute | solution.py:50
  75.2 9.0 %collective-permute-start.19 = (bf16[8,24,512]{2,1,0:T(8,128)(2,1)S(1)}, bf16[8,24,512]{2,1,0:T(8,128)(2,1)S(1)}, u32[]{:S(2)}, u32[]{:S(2)}) collective-permute-start(bf16[8,24,512]{2,1,0:T(8,128)(2,1)S(1)} %collective-permute-done.15.refs_1_), channel_id=1, source_target_pairs={{0,2},{2,0},{4,6},{6,4},{8,10},{10,8},{12,14},{14,12},{1,3},{3,1},... | collective-permute-start | bytes 589832 | tf_op jit(solution)/shard_map/ppermute | solution.py:46
  76.3 11.0 %collective-permute-start.24 = (bf16[8,24,512]{2,1,0:T(8,128)(2,1)S(1)}, bf16[8,24,512]{2,1,0:T(8,128)(2,1)S(1)}, u32[]{:S(2)}, u32[]{:S(2)}) collective-permute-start(bf16[8,24,512]{2,1,0:T(8,128)(2,1)S(1)} %collective-permute-done.16.refs_2_), channel_id=1, source_target_pairs={{1,0},{0,1},{3,2},{2,3},{5,4},{4,5},{7,6},{6,7},{9,8},{8,9},{11,10... | collective-permute-start | bytes 589832 | tf_op jit(solution)/shard_map/ppermute | solution.py:50
  80.0 13.4 %collective-permute-start.26 = (bf16[8,24,512]{2,1,0:T(8,128)(2,1)S(1)}, bf16[8,24,512]{2,1,0:T(8,128)(2,1)S(1)}, u32[]{:S(2)}, u32[]{:S(2)}) collective-permute-start(bf16[8,24,512]{2,1,0:T(8,128)(2,1)S(1)} %collective-permute-done.22.refs_0_), channel_id=1, source_target_pairs={{0,2},{2,0},{4,6},{6,4},{8,10},{10,8},{12,14},{14,12},{1,3},{3,1},... | collective-permute-start | bytes 589832 | tf_op jit(solution)/shard_map/ppermute | solution.py:46
  80.0 7.6 %collective-permute-start.20 = (bf16[8,24,512]{2,1,0:T(8,128)(2,1)S(1)}, bf16[8,24,512]{2,1,0:T(8,128)(2,1)S(1)}, u32[]{:S(2)}, u32[]{:S(2)}) collective-permute-start(bf16[8,24,512]{2,1,0:T(8,128)(2,1)S(1)} %collective-permute-done.16.refs_2_), channel_id=1, source_target_pairs={{0,2},{2,0},{4,6},{6,4},{8,10},{10,8},{12,14},{14,12},{1,3},{3,1},... | collective-permute-start | bytes 589832 | tf_op jit(solution)/shard_map/ppermute | solution.py:46
  84.2 9.2 %collective-permute-start.29 = (bf16[8,24,512]{2,1,0:T(8,128)(2,1)S(1)}, bf16[8,24,512]{2,1,0:T(8,128)(2,1)S(1)}, u32[]{:S(2)}, u32[]{:S(2)}) collective-permute-start(bf16[8,24,512]{2,1,0:T(8,128)(2,1)S(1)} %collective-permute-done.25.refs_3_), channel_id=1, source_target_pairs={{0,2},{2,0},{4,6},{6,4},{8,10},{10,8},{12,14},{14,12},{1,3},{3,1},... | collective-permute-start | bytes 589832 | tf_op jit(solution)/shard_map/ppermute | solution.py:46
  84.2 9.2 %collective-permute-start.27 = (bf16[8,24,512]{2,1,0:T(8,128)(2,1)S(1)}, bf16[8,24,512]{2,1,0:T(8,128)(2,1)S(1)}, u32[]{:S(2)}, u32[]{:S(2)}) collective-permute-start(bf16[8,24,512]{2,1,0:T(8,128)(2,1)S(1)} %collective-permute-done.23.refs_1_), channel_id=1, source_target_pairs={{0,2},{2,0},{4,6},{6,4},{8,10},{10,8},{12,14},{14,12},{1,3},{3,1},... | collective-permute-start | bytes 589832 | tf_op jit(solution)/shard_map/ppermute | solution.py:46
  87.3 6.1 %collective-permute-start.28 = (bf16[8,24,512]{2,1,0:T(8,128)(2,1)S(1)}, bf16[8,24,512]{2,1,0:T(8,128)(2,1)S(1)}, u32[]{:S(2)}, u32[]{:S(2)}) collective-permute-start(bf16[8,24,512]{2,1,0:T(8,128)(2,1)S(1)} %collective-permute-done.24.refs_2_), channel_id=1, source_target_pairs={{0,2},{2,0},{4,6},{6,4},{8,10},{10,8},{12,14},{14,12},{1,3},{3,1},... | collective-permute-start | bytes 589832 | tf_op jit(solution)/shard_map/ppermute | solution.py:46
  105.1 2.5 %collective-permute-start.35 = (bf16[2,4,24,2048]{3,2,1,0:T(8,128)(2,1)S(1)}, bf16[2,4,24,2048]{3,2,1,0:T(8,128)(2,1)S(1)}, u32[]{:S(2)}, u32[]{:S(2)}) collective-permute-start(bf16[2,4,24,2048]{3,2,1,0:T(8,128)(2,1)S(1)} %get-tuple-element.19), channel_id=1, source_target_pairs={{0,2},{2,0},{4,6},{6,4},{8,10},{10,8},{12,14},{14,12},{1,3},{3,1},... | collective-permute-start | bytes 2359304 | tf_op jit(solution)/shard_map/ppermute | solution.py:46
  105.6 4.5 %collective-permute-start.30 = (bf16[2,4,24,2048]{3,2,1,0:T(8,128)(2,1)S(1)}, bf16[2,4,24,2048]{3,2,1,0:T(8,128)(2,1)S(1)}, u32[]{:S(2)}, u32[]{:S(2)}) collective-permute-start(bf16[2,4,24,2048]{3,2,1,0:T(8,128)(2,1)S(1)} %get-tuple-element.16), channel_id=1, source_target_pairs={{0,2},{2,0},{4,6},{6,4},{8,10},{10,8},{12,14},{14,12},{1,3},{3,1},... | collective-permute-start | bytes 2359304 | tf_op jit(solution)/shard_map/ppermute | solution.py:46
  107.8 7.5 %collective-permute-start.36 = (bf16[2,24,2048]{2,1,0:T(8,128)(2,1)S(1)}, bf16[2,24,2048]{2,1,0:T(8,128)(2,1)S(1)}, u32[]{:S(2)}, u32[]{:S(2)}) collective-permute-start(bf16[2,24,2048]{2,1,0:T(8,128)(2,1)S(1)} %get-tuple-element.37), channel_id=1, source_target_pairs={{0,8},{2,10},{4,0},{6,2},{8,12},{10,14},{12,4},{14,6},{1,9},{3,11}... | collective-permute-start | bytes 589832 | tf_op jit(solution)/shard_map/ppermute | solution.py:42
  110.3 11.2 %collective-permute-start.31 = (bf16[4,24,2048]{2,1,0:T(8,128)(2,1)S(1)}, bf16[4,24,2048]{2,1,0:T(8,128)(2,1)S(1)}, u32[]{:S(2)}, u32[]{:S(2)}) collective-permute-start(bf16[4,24,2048]{2,1,0:T(8,128)(2,1)S(1)} %fusion.3), channel_id=1, source_target_pairs={{1,0},{0,1},{3,2},{2,3},{5,4},{4,5},{7,6},{6,7},{9,8},{8,9},{11,10... | collective-permute-start | bytes 1179656 | tf_op jit(solution)/shard_map/ppermute | solution.py:50
  111.9 13.3 %collective-permute-start.38 = (bf16[2,24,2048]{2,1,0:T(8,128)(2,1)S(1)}, bf16[2,24,2048]{2,1,0:T(8,128)(2,1)S(1)}, u32[]{:S(2)}, u32[]{:S(2)}) collective-permute-start(bf16[2,24,2048]{2,1,0:T(8,128)(2,1)S(1)} %get-tuple-element.38), channel_id=1, source_target_pairs={{0,4},{2,6},{4,12},{6,14},{8,0},{10,2},{12,8},{14,10},{1,5},{3,7},... | collective-permute-start | bytes 589832 | tf_op jit(solution)/shard_map/ppermute | solution.py:42
  115.4 9.8 %collective-permute-start.37 = (bf16[2,24,2048]{2,1,0:T(8,128)(2,1)S(1)}, bf16[2,24,2048]{2,1,0:T(8,128)(2,1)S(1)}, u32[]{:S(2)}, u32[]{:S(2)}) collective-permute-start(bf16[2,24,2048]{2,1,0:T(8,128)(2,1)S(1)} %fusion.5), channel_id=1, source_target_pairs={{0,8},{2,10},{4,0},{6,2},{8,12},{10,14},{12,4},{14,6},{1,9},{3,11}... | collective-permute-start | bytes 589832 | tf_op jit(solution)/shard_map/ppermute | solution.py:42
  121.6 5.4 %collective-permute-start.32 = (bf16[1,24,2048]{2,1,0:T(8,128)(2,1)S(1)}, bf16[1,24,2048]{2,1,0:T(8,128)(2,1)S(1)}, u32[]{:S(2)}, u32[]{:S(2)}) collective-permute-start(bf16[1,24,2048]{2,1,0:T(8,128)(2,1)S(1)} %get-tuple-element.39), channel_id=1, source_target_pairs={{0,8},{2,10},{4,0},{6,2},{8,12},{10,14},{12,4},{14,6},{1,9},{3,11}... | collective-permute-start | bytes 294920 | tf_op jit(solution)/shard_map/ppermute | solution.py:42
  122.7 7.3 %collective-permute-start.34 = (bf16[1,24,2048]{2,1,0:T(8,128)(2,1)S(1)}, bf16[1,24,2048]{2,1,0:T(8,128)(2,1)S(1)}, u32[]{:S(2)}, u32[]{:S(2)}) collective-permute-start(bf16[1,24,2048]{2,1,0:T(8,128)(2,1)S(1)} %get-tuple-element.40), channel_id=1, source_target_pairs={{0,4},{2,6},{4,12},{6,14},{8,0},{10,2},{12,8},{14,10},{1,5},{3,7},... | collective-permute-start | bytes 294920 | tf_op jit(solution)/shard_map/ppermute | solution.py:42
  125.3 4.7 %collective-permute-start.39 = (bf16[1,24,2048]{2,1,0:T(8,128)(2,1)S(1)}, bf16[1,24,2048]{2,1,0:T(8,128)(2,1)S(1)}, u32[]{:S(2)}, u32[]{:S(2)}) collective-permute-start(bf16[1,24,2048]{2,1,0:T(8,128)(2,1)S(1)} %slice.119), channel_id=1, source_target_pairs={{1,0},{0,1},{3,2},{2,3},{5,4},{4,5},{7,6},{6,7},{9,8},{8,9},{11,10... | collective-permute-start | bytes 294920 | tf_op jit(solution)/shard_map/ppermute | solution.py:50
  127.1 4.8 %collective-permute-start.33 = (bf16[1,24,2048]{2,1,0:T(8,128)(2,1)S(1)}, bf16[1,24,2048]{2,1,0:T(8,128)(2,1)S(1)}, u32[]{:S(2)}, u32[]{:S(2)}) collective-permute-start(bf16[1,24,2048]{2,1,0:T(8,128)(2,1)S(1)} %fusion.12), channel_id=1, source_target_pairs={{0,8},{2,10},{4,0},{6,2},{8,12},{10,14},{12,4},{14,6},{1,9},{3,11}... | collective-permute-start | bytes 294920 | tf_op jit(solution)/shard_map/ppermute | solution.py:42

commit v2 on v1

v2 whole, which is shorter than its diff:
```python
import functools
import math

import jax
import jax.numpy as jnp
from jax import lax
from jax.experimental import pallas as pl
from jax.experimental.pallas import tpu as pltpu
from jax.sharding import PartitionSpec as P

HEAD_SIZE = 128
CORES = 2
BF16 = jnp.bfloat16
F32 = jnp.float32


NT = (((1,), (1,)), ((), ()))


def fold_order(count):
    return list(range(0, count, 2)) + list(range(count - 1 - count % 2, 0, -2))


def chip_perm(chips, shift):
    order = fold_order(chips)
    place = {z: i for i, z in enumerate(order)}
    to = lambda z: order[(place[z] + shift) % chips]
    return [(z * CORES + c, to(z) * CORES + c) for z in range(chips) for c in range(CORES)]


def core_perm(chips):
    return [(z * CORES + c, z * CORES + 1 - c) for z in range(chips) for c in range(CORES)]


def chip_table(chips, sign):
    order = fold_order(chips)
    place = {z: i for i, z in enumerate(order)}
    return [[order[(place[z] + sign * s) % chips] for s in range(chips)] for z in range(chips)]


def chip_send(piece, chips, shift):
    return lax.ppermute(piece, "expert", chip_perm(chips, shift))


def core_swap(piece, chips):
    return lax.ppermute(piece, "expert", core_perm(chips))


def tensor_shift(piece, tensors, shift):
    return lax.ppermute(piece, "tensor", [((i + shift) % tensors, i) for i in range(tensors)])


def chip_gather(piece, chips):
    pieces = [None] * chips
    pieces[0] = piece
    ahead = back = piece
    for s in range(1, chips // 2 + 1):
        if pieces[s] is None:
            ahead = chip_send(ahead, chips, 1)
            pieces[s] = ahead
        if pieces[chips - s] is None:
            back = chip_send(back, chips, -1)
            pieces[chips - s] = back
    return pieces


def chip_scatter(pieces, chips):
    arrived = []
    for sign, steps in ((1, chips // 2), (-1, (chips - 1) // 2)):
        held = None
        for s in range(steps, 0, -1):
            own = pieces[s if sign > 0 else chips - s]
            held = own if held is None else add(own, held)
            held = chip_send(held, chips, sign)
        if held is not None:
            arrived.append(held)
    return arrived


def attention_kernel(
    chunk, kv_heads, head_count, tab_ref, len_ref, q_ref, new_ref, cache_ref, out_ref, qs, buf, sems
):
    rows = q_ref.shape[1]
    group = head_count // kv_heads
    factor = 1.0 / math.sqrt(HEAD_SIZE)
    first = tab_ref[0] * rows
    pitch = qs.shape[0] // rows

    copies = []
    for c in range(rows // chunk):
        copies.append(
            pltpu.make_async_copy(
                cache_ref.at[pl.ds(first + c * chunk, chunk)],
                buf.at[pl.ds(c * chunk, chunk)],
                sems.at[c],
            )
        )
        copies[-1].start()
    for h in range(head_count):
        qs[pl.ds(h, rows, stride=pitch), :] = q_ref[
            0, :, h * HEAD_SIZE : (h + 1) * HEAD_SIZE
        ].astype(F32)

    positions = buf.shape[2]
    block = chunk * head_count
    pos = lax.broadcasted_iota(jnp.int32, (head_count, positions), 1)
    head_kv = lax.broadcasted_iota(jnp.int32, (block, HEAD_SIZE), 0) // group % kv_heads
    wide = (head_count, new_ref.shape[3])
    for c in range(rows // chunk):
        span = range(c * chunk, (c + 1) * chunk)
        q32 = jnp.concatenate([qs[t * pitch : t * pitch + head_count, :] for t in span], axis=0)
        spread = [jnp.where(head_kv == kv, q32, 0.0) for kv in range(kv_heads)]
        q = spread[0] if kv_heads == 1 else jnp.concatenate(spread, axis=1)
        q16 = q.astype(BF16)
        keys = [jnp.broadcast_to(new_ref[0, t, 0:1, :].astype(F32), wide) for t in span]
        values = [jnp.broadcast_to(new_ref[0, t, 1:2, :].astype(F32), wide) for t in span]
        own = jnp.sum(q * jnp.concatenate(keys, axis=0), axis=1, keepdims=True) * factor
        copies[c].wait()
        scores = []
        for i, t in enumerate(span):
            score = lax.dot_general(
                q16[i * head_count : (i + 1) * head_count],
                buf[t, 0],
                NT,
                preferred_element_type=F32,
            )
            scores.append(jnp.where(pos < len_ref[first + t], score * factor, -jnp.inf))
        scores = jnp.concatenate(scores, axis=0)
        highest = jnp.maximum(jnp.max(scores, axis=1, keepdims=True), own)
        weights = jnp.exp(scores - highest)
        own_weight = jnp.exp(own - highest)
        inverse = 1.0 / (jnp.sum(weights, axis=1, keepdims=True) + own_weight)
        probs = (weights * inverse).astype(BF16)
        own_prob = (own_weight * inverse).astype(BF16).astype(F32)
        mixed = jnp.concatenate(
            [
                jnp.dot(
                    probs[i * head_count : (i + 1) * head_count],
                    buf[t, 1],
                    preferred_element_type=F32,
                )
                for i, t in enumerate(span)
            ],
            axis=0,
        )
        mixed = mixed + own_prob * jnp.concatenate(values, axis=0)
        out = mixed[:, :HEAD_SIZE]
        for kv in range(1, kv_heads):
            out = jnp.where(head_kv == kv, mixed[:, kv * HEAD_SIZE : (kv + 1) * HEAD_SIZE], out)
        for i, t in enumerate(span):
            qs[t * pitch : t * pitch + head_count, :] = out[i * head_count : (i + 1) * head_count]

    for h in range(head_count):
        out_ref[:, h * HEAD_SIZE : (h + 1) * HEAD_SIZE] = qs[
            pl.ds(h, rows, stride=pitch), :
        ].astype(BF16)


def attend(part, query, latest, cache, lengths, parts):
    token_count, width = query.shape
    rows = token_count // parts
    kv_width = latest.shape[2]
    kv_heads = kv_width // HEAD_SIZE
    head_count = width // HEAD_SIZE
    chunk = next(k for k in (8, 6, 4, 3, 2, 1) if rows % k == 0)
    return pl.pallas_call(
        functools.partial(attention_kernel, chunk, kv_heads, head_count),
        grid_spec=pltpu.PrefetchScalarGridSpec(
            num_scalar_prefetch=2,
            grid=(1,),
            in_specs=[
                pl.BlockSpec((1, rows, width), lambda i, tab, ln: (tab[0], 0, 0)),
                pl.BlockSpec((1, rows, 2, kv_width), lambda i, tab, ln: (tab[0], 0, 0, 0)),
                pl.BlockSpec(memory_space=pltpu.HBM),
            ],
            out_specs=pl.BlockSpec((rows, width), lambda i, tab, ln: (0, 0)),
            scratch_shapes=[
                pltpu.VMEM((rows * (head_count + 8), HEAD_SIZE), F32),
                pltpu.VMEM((rows,) + cache.shape[1:], BF16),
                pltpu.SemaphoreType.DMA((rows // chunk,)),
            ],
        ),
        out_shape=jax.ShapeDtypeStruct((rows, width), BF16),
        compiler_params=pltpu.CompilerParams(
            dimension_semantics=("arbitrary",), vmem_limit_bytes=12 << 20
        ),
        name="attend",
    )(
        part.reshape(1),
        *in_hbm(
            lengths,
            query.reshape(parts, rows, width),
            latest.reshape(parts, rows, 2, kv_width),
            cache,
        ),
    )


def in_hbm(*arrays):
    return [pltpu.with_memory_space_constraint(a, pltpu.HBM) for a in arrays]


def on_chip(*arrays):
    return [pltpu.with_memory_space_constraint(a, pltpu.VMEM) for a in arrays]


def project_kernel(count, steps, add_count, tab_ref, *refs):
    pieces, w_ref = refs[:count], refs[count]
    adds = refs[count + 1 : count + 1 + add_count]
    rows, width = pieces[0].shape
    columns = w_ref.shape[1]
    if steps:
        out_ref, buf, sems = refs[-3:]
        deep = width // steps
        copies = [
            pltpu.make_async_copy(
                w_ref.at[pl.ds(k * deep, deep)], buf.at[pl.ds(k * deep, deep)], sems.at[k]
            )
            for k in range(steps)
        ]
        for copy in copies:
            copy.start()
    else:
        out_ref, buf = refs[-1], w_ref
    lhs = jnp.concatenate([p[...].astype(F32) for p in pieces], axis=0).astype(BF16)
    if steps:
        for copy in copies:
            copy.wait()
    result = jnp.dot(lhs, buf[...], preferred_element_type=F32)
    for i in range(count):
        block = tab_ref[i]
        value = result[i * rows : (i + 1) * rows]
        for a in adds:
            value = value + a[block][:, :columns].astype(F32)
        out_ref[block] = value.astype(BF16)


def project(table, pieces, w_out, adds, given, resident):
    rows, _ = pieces[0].shape
    count = len(pieces)
    steps = 0 if resident else 4
    vmem = pl.BlockSpec(memory_space=pltpu.VMEM)
    hbm = pl.BlockSpec(memory_space=pltpu.HBM)
    shapes = [jax.ShapeDtypeStruct((count, rows, w_out.shape[1]), BF16)]
    if not resident:
        shapes.append(pltpu.VMEM(w_out.shape, BF16))
    operands = adds if adds else [given]
    made = pl.pallas_call(
        functools.partial(project_kernel, count, steps, len(adds)),
        in_specs=[pl.BlockSpec(memory_space=pltpu.SMEM)]
        + [vmem] * count
        + [vmem if resident else hbm]
        + [vmem] * len(operands),
        out_specs=[vmem] * len(shapes),
        out_shape=shapes,
        scratch_shapes=[pltpu.SemaphoreType.DMA((steps,))] if steps else [],
        compiler_params=pltpu.CompilerParams(vmem_limit_bytes=16 << 20),
        name="project",
    )(table, *pieces, *(on_chip if resident else in_hbm)(w_out), *operands)
    return made[0], w_out if resident else made[1]


def down_product(acts, wd_buf, tab_ref, outs):
    local, hidden, features = wd_buf.shape
    chips = acts[0].shape[1]
    count = chips * CORES
    core = tab_ref[count + 1]
    aligned = hidden % 128 == 0
    left = []
    for e in range(local):
        picked = [
            act[e, tab_ref[count + 2 + s], half].astype(F32)
            for half in (1 - core, core)
            for act in acts
            for s in range(chips)
        ]
        left.append(jnp.concatenate(picked, axis=0).astype(BF16))
    if aligned:
        left = [jnp.concatenate(left, axis=1)]
    rows = left[0].shape[0] // 2
    wide = features * 2 // len(outs)
    block = min(wide, 1024)
    for first in range(0, features, block):
        source = slice(first, first + block)
        if aligned:
            right = [wd_buf[:, :, source].reshape(local * hidden, block)]
        else:
            right = [wd_buf[e, :, source] for e in range(local)]
        result = sum(jnp.dot(l, r, preferred_element_type=F32) for l, r in zip(left, right))
        result = result.astype(BF16)
        span = slice(first % wide, first % wide + block)
        for k in range(2):
            out_ref = outs[first // wide * 2 + k]
            value = result[k * rows : (k + 1) * rows].reshape(out_ref.shape[:3] + (block,))
            out_ref[:, :, :, span] = value


def up_kernel(jobs, acts_in, pieces, resident, count, tab_ref, *refs):
    refs = list(refs)
    take = lambda k: [refs.pop(0) for _ in range(k)]
    slices = [dict(zip(picked, take(len(picked)))) for _, picked, _, _ in jobs]
    starts = [take(2) if begun else None for _, _, begun, _ in jobs]
    gain_ref, weight_ref = take(2)
    acts = take(acts_in)
    wg_ref, wu_ref, wd_ref = take(3)
    results = [take(1 if ended else 2) for _, _, _, ended in jobs if not (ended and pieces)]
    own_ref = take(1)[0] if jobs[0][0] == 0 else None
    outs = take(2 * pieces)
    if resident:
        wg_buf, wu_buf, wd_buf = wg_ref, wu_ref, wd_ref
    else:
        wg_buf, wu_buf, wd_buf, sems = take(4)
    if pieces:
        results = [take(1)] + results
    local, features, hidden = wg_ref.shape
    _, rows, columns = next(iter(slices[0].values())).shape
    total = count * rows
    aligned = hidden % 128 == 0
    used = sorted(set(i for _, picked, _, _ in jobs for i in picked))

    def span_of(i):
        return pl.ds(pl.multiple_of(tab_ref[i] * columns, columns), columns)

    copies = {}
    if not resident:
        copies = {
            i: [
                pltpu.make_async_copy(
                    src.at[:, span_of(i), :], dst.at[:, span_of(i), :], sems.at[k, i]
                )
                for k, (src, dst) in enumerate(((wg_ref, wg_buf), (wu_ref, wu_buf)))
            ]
            for i in range(count)
        }
        down = pltpu.make_async_copy(wd_ref, wd_buf, sems.at[2, 0])
        for i in copies:
            for copy in copies[i]:
                copy.start()
        down.start()
    sums, squares = [], []
    for begun in starts:
        if begun is None:
            sums.append(None)
            squares.append(jnp.zeros((total, 1), F32))
        else:
            parts = [begun[0][k] for k in range(2 * local)]
            sums.append([jnp.concatenate(parts, axis=1)] if aligned else parts)
            squares.append(begun[1][...])
    for i in used:
        span = span_of(i)
        gain = gain_ref[:, span].astype(F32)
        left = {}
        for n, held in enumerate(slices):
            if i in held:
                x = held[i][...].astype(F32).reshape(total, columns)
                squares[n] = squares[n] + jnp.sum(x * x, axis=1, keepdims=True)
                left[n] = (x * gain).astype(BF16)
                if jobs[n][0] == 0:
                    own_ref[:, span] = held[i][tab_ref[count]]
        for copy in copies.get(i, ()):
            copy.wait()
        weights = [w[e, span, :] for w in (wg_buf, wu_buf) for e in range(local)]
        if aligned:
            weights = [jnp.concatenate(weights, axis=1)]
        both = jnp.concatenate(list(left.values()), axis=0) if len(left) > 1 else left[next(iter(left))]
        both = [jnp.dot(both, w, preferred_element_type=F32) for w in weights]
        for k, n in enumerate(left):
            more = [b[k * total : (k + 1) * total] for b in both]
            sums[n] = more if sums[n] is None else [a + b for a, b in zip(sums[n], more)]
    for n, (part, _, _, ended) in enumerate(jobs):
        final = sums[n]
        if aligned:
            final = [final[0][:, k * hidden : (k + 1) * hidden] for k in range(2 * local)]
        if not ended:
            for k in range(2 * local):
                results[n][0][k] = final[k]
            results[n][1][...] = squares[n]
            continue
        act_ref = results[n][0]
        scale = lax.rsqrt(squares[n] * (1.0 / features) + 1e-06)
        for e in range(local):
            gate = final[e] * scale
            up = final[local + e] * scale
            chosen = weight_ref[part, :, e : e + 1]
            value = gate / (1.0 + jnp.exp(-gate)) * up * chosen
            value = jnp.where(chosen != 0.0, value, 0.0).astype(BF16)
            for i in range(count):
                act_ref[e, i // CORES, i % CORES] = value[i * rows : (i + 1) * rows]
        acts.append(act_ref)
    if not resident:
        down.wait()
    if pieces:
        down_product(acts, wd_buf, tab_ref, outs)


def expert_up(table, jobs, held, begun, gain, weights, matrices, acts, pieces, resident):
    count = len(held[0])
    local, features, hidden = matrices[0].shape
    _, rows, _ = held[0][0].shape
    chips = count // CORES
    vmem = pl.BlockSpec(memory_space=pltpu.VMEM)
    hbm = pl.BlockSpec(memory_space=pltpu.HBM)
    inputs, shapes = [], []
    for part, picked, _, _ in jobs:
        inputs += [held[part][i] for i in picked]
    for _, _, has, _ in jobs:
        inputs += list(begun) if has else []
    inputs += [gain.reshape(1, -1), weights]
    for part, _, _, ended in jobs:
        if ended:
            act_shape = (local, chips, CORES, rows, hidden)
            if not pieces:
                shapes.append(jax.ShapeDtypeStruct(act_shape, BF16))
        else:
            shapes.append(jax.ShapeDtypeStruct((2 * local, count * rows, hidden), F32))
            shapes.append(jax.ShapeDtypeStruct((count * rows, 1), F32))
    if jobs[0][0] == 0:
        shapes.append(jax.ShapeDtypeStruct((rows, features), BF16))
    inputs += acts
    specs = [vmem] * len(inputs) + [vmem if resident else hbm] * 3
    inputs += (on_chip if resident else in_hbm)(*matrices)
    if pieces:
        parts = len(acts) + sum(ended for _, _, _, ended in jobs)
        shape = jax.ShapeDtypeStruct((parts, chips, rows, features // pieces), BF16)
        shapes += [shape] * (2 * pieces)
    scratch = []
    if not resident:
        shapes += [pltpu.VMEM(m.shape, BF16) for m in matrices]
        scratch.append(pltpu.SemaphoreType.DMA((3, count)))
    if pieces:
        scratch.append(pltpu.VMEM(act_shape, BF16))
    return pl.pallas_call(
        functools.partial(up_kernel, jobs, len(acts), pieces, resident, count),
        in_specs=[pl.BlockSpec(memory_space=pltpu.SMEM)] + specs,
        out_specs=[vmem] * len(shapes),
        out_shape=shapes,
        scratch_shapes=scratch,
        compiler_params=pltpu.CompilerParams(vmem_limit_bytes=20 << 20),
        name="expert_up",
    )(table, *inputs)


def add_kernel(split, *refs):
    left, right = refs[0], refs[1]
    for k, out_ref in enumerate(refs[2:]):
        if split is None:
            out_ref[...] = (left[...].astype(F32) + right[...].astype(F32)).astype(out_ref.dtype)
            continue
        at = (k,) if split == 0 else (slice(None), k)
        out_ref[...] = (left[at].astype(F32) + right[at].astype(F32)).astype(out_ref.dtype)


def add(left, right, split=None):
    vmem = pl.BlockSpec(memory_space=pltpu.VMEM)
    if split is None:
        shapes = [jax.ShapeDtypeStruct(left.shape, BF16)]
    else:
        shape = left.shape[:split] + left.shape[split + 1 :]
        shapes = [
            jax.ShapeDtypeStruct(shape, F32 if k == 0 else BF16) for k in range(left.shape[split])
        ]
    result = pl.pallas_call(
        functools.partial(add_kernel, split),
        in_specs=[vmem] * 2,
        out_specs=[vmem] * len(shapes),
        out_shape=shapes,
        compiler_params=pltpu.CompilerParams(vmem_limit_bytes=12 << 20),
        name="add",
    )(left, right)
    return result[0] if split is None else result


def per_device(
    query,
    latest_key_value,
    cache,
    lengths,
    w_out,
    residual_in,
    norm_gain,
    expert_ids,
    route_weights,
    w_gate,
    w_up,
    w_down,
):
    count = lax.axis_size("expert")
    tensors = lax.axis_size("tensor")
    chips = count // CORES
    me = lax.axis_index("expert")
    mine = lax.axis_index("tensor")
    core = me % CORES
    chip = me // CORES
    token_count = query.shape[0]
    rows = token_count // tensors
    columns = w_out.shape[1]
    local = w_gate.shape[0]

    behind = jnp.take(jnp.array(chip_table(chips, -1), jnp.int32), chip, axis=0)
    ahead = jnp.take(jnp.array(chip_table(chips, 1), jnp.int32), chip, axis=0)
    blocks = jnp.concatenate([behind * CORES + core, behind * CORES + (1 - core)])
    table = jnp.concatenate([blocks, me[None], core[None], ahead]).astype(jnp.int32)

    named = expert_ids[:, :, None] == jnp.arange(local * count, dtype=jnp.int32)
    dense = jnp.sum(jnp.where(named, route_weights[:, :, None], 0.0), axis=1)
    high = dense.astype(BF16)
    low = (dense - high.astype(F32)).astype(BF16)
    pair = jnp.stack([high, low], axis=-1).reshape(tensors, rows, count, local * 2)
    pair = jnp.roll(pair, -mine, axis=0)
    pair = pair.transpose(2, 1, 0, 3).reshape(count, rows, tensors * local * 2)
    pair = jnp.pad(pair, ((0, 0), (0, 0), (0, 128 - pair.shape[2])))
    shares = residual_in.reshape(rows, count, columns).transpose(1, 0, 2)
    packed = jnp.concatenate([shares, pair], axis=2)
    given = lax.all_to_all(packed, "expert", split_axis=0, concat_axis=0, tiled=True)
    pair = given[:, :, columns : columns + tensors * local * 2].astype(F32)
    pair = pair.reshape(count, rows, tensors, local, 2).sum(axis=-1)
    weights = pair.transpose(2, 0, 1, 3).reshape(tensors, count * rows, local)

    passed = []
    for j in range(1, tensors + 1):
        part = (mine + j) % tensors
        attended = attend(part, query, latest_key_value, cache, lengths, tensors)
        pieces = chip_gather(attended, chips)
        pieces = pieces + [core_swap(p, chips) for p in pieces]
        adds = [] if j < tensors else passed + [given]
        stream, w_out = project(table, pieces, w_out, adds, given, j > 1)
        if j < tensors:
            passed.append(tensor_shift(stream, tensors, -j))

    gathered = chip_gather(stream, chips)
    held = []
    for j in range(tensors):
        rows_of = gathered
        if j:
            rows_of = [tensor_shift(p, tensors, j) for p in gathered]
        held.append(rows_of + [core_swap(p, chips) for p in rows_of])

    everything = tuple(range(count))
    early = tuple(i for i in everything if i % chips < 2) if tensors > 1 else ()
    late = tuple(i for i in everything if i not in early)
    final = tensors - 1
    matrices = [w_gate, w_up, w_down]
    acts, begun = [], ()
    for j in range(tensors):
        jobs = [(j, late if early and j == final else everything, bool(early) and j == final, True)]
        if j == 0 and early:
            jobs.append((final, early, False, False))
        pieces = 2 if j == final else 0
        made = list(
            expert_up(
                table, jobs, held, begun, norm_gain, weights, matrices,
                acts if pieces else [], pieces, j > 0,
            )
        )
        if not pieces:
            acts.append(made.pop(0))
        if len(jobs) > 1:
            begun = (made.pop(0), made.pop(0))
        if j == 0:
            mine_rows = made.pop(0)
            matrices = made[2 * pieces :]

    swapped = [core_swap(made[2 * p], chips) for p in range(2)]
    sums = []
    for p, split in enumerate((1, 0)):
        first = add(made[2 * p + 1], swapped[p], split)
        if split == 1:
            total = first[0]
            for moved in chip_scatter(first, chips):
                total = total + moved.astype(F32)
            kept = total[0]
            for j in range(1, tensors):
                moved = tensor_shift(total[j].astype(BF16), tensors, -j)
                kept = kept + moved.astype(F32)
        else:
            kept = first[0]
            for j in range(1, tensors):
                moved = tensor_shift(first[j], tensors, -j)
                if j < tensors - 1:
                    kept = kept + moved.astype(F32)
            if tensors > 1:
                first = add(kept, moved, 0)
            else:
                first = [kept[0]] + [kept[s].astype(BF16) for s in range(1, chips)]
            kept = first[0]
            for moved in chip_scatter(first, chips):
                kept = kept + moved.astype(F32)
        sums.append(kept)
    return (mine_rows.astype(F32) + jnp.concatenate(sums, axis=1)).astype(BF16)


def solution(mesh):
    placed = (
        P(("groups", "expert"), "tensor"),
        P(("groups", "expert"), None, "tensor"),
        P(("groups", "expert"), None, None, "tensor"),
        P(("groups", "expert")),
        P("tensor", "expert"),
        P(("groups", "expert", "tensor"), None),
        P(),
        P(("groups", "expert"), None),
        P(("groups", "expert"), None),
        P("expert", None, "tensor"),
        P("expert", None, "tensor"),
        P("expert", "tensor", None),
    )

    return jax.shard_map(
        per_device,
        mesh=mesh,
        in_specs=placed,
        out_specs=P(("groups", "expert", "tensor"), None),
        check_vma=False,
    )
```

time: 133 us -> 129 us (0.970)
  Pallas kernels: 33.8 us -> 27.5 us
  starting transfers between devices: 42.9 us -> 46 us
    pallas_call x5 -> x9, Pallas kernels: 24.6 us -> 17.9 us  [the longest x2 12.1 us: expert_up(): pl.pallas_call(functools.partial(up_kernel, jobs, len(acts), pieces, resi...]
    ppermute x15, starting transfers between devices: 27.1 us -> 31.7 us  [chip_send(): return lax.ppermute(piece, 'expert', chip_perm(chips, shift))]
    ppermute x15, waiting for transfers between devices: 31.3 us -> 32.9 us  [chip_send(): return lax.ppermute(piece, 'expert', chip_perm(chips, shift))]
  transfers between devices with their start and end apart: 41 -> 41, of which waited for: 16 -> 16; matrix products, arithmetic and copies ran while one was open for 3% -> 2% of each run, Pallas kernels for 11% -> 13%
where the time goes in v2:
time: 129 us
  waiting for transfers between devices  51.1 us (40%)
  starting transfers between devices  46 us (36%)
  Pallas kernels  27.5 us (21%)
  other arithmetic  3.07 us (2%)
    ppermute x15, waiting for transfers between devices, chip_send(): return lax.ppermute(piece, 'expert', chip_perm(chips, shift))  32.9 us
    ppermute x15, starting transfers between devices, chip_send(): return lax.ppermute(piece, 'expert', chip_perm(chips, shift))  31.7 us
    ppermute x7, waiting for transfers between devices, tensor_shift(): lax.ppermute(piece, 'tensor', [((i + shift) % tensors, i) for i in range(...  16.3 us
    pallas_call x2, Pallas kernels, expert_up(): pl.pallas_call(functools.partial(up_kernel, jobs, len(acts), pieces, resi...  12.1 us
    pallas_call x2, Pallas kernels, attend(): pl.pallas_call(functools.partial(attention_kernel, chunk, kv_heads, head_...  9.6 us
    ppermute x7, starting transfers between devices, tensor_shift(): lax.ppermute(piece, 'tensor', [((i + shift) % tensors, i) for i in range(...  8.58 us
    pallas_call x2, Pallas kernels, project(): pl.pallas_call(functools.partial(project_kernel, count, steps, len(adds))...  5.32 us
    all_to_all x1, starting transfers between devices, per_device(): lax.all_to_all(packed, 'expert', split_axis=0, concat_axis=0, tiled=True)  3.41 us
  transfers between devices with their start and end apart: 41, of which 16 were waited for; matrix products, arithmetic and copies ran while one was open for 2% of the time, Pallas kernels for 13%

profile of v2, /device:TPU:0, one launch (start us, length us, event | category | flops | bytes accessed | tf_op | source)
XLA Modules:
  0.0 128.5 jit_solution(18201726865059700026)
XLA Ops:
  0.0 4.9 %attend.3.refs_0_ = bf16[24,4096]{1,0:T(8,128)(2,1)S(1)} custom-call(s32[1]{0:T(128)} %bitcast.7.tab_ref, s32[48]{0:T(128)} %len_ref.3, bf16[2,24,4096]{2,1,0:T(8,128)(2,1)} %bitcast.46, bf16[2,24,2,256]{3,2,1,0:T(2,128)(2,1)} %bitcast.49, bf16[48,2,128,256]{3,2,1,0:T(8,128)(2,1)} %cache_ref.3), custom_call_target="tpu_custom_call" | custom-call | tf_op jit(solution)/shard_map/attend/pallas_call | solution.py:166
  4.9 4.1 %collective-permute-start.7 = (bf16[24,4096]{1,0:T(8,128)(2,1)S(1)}, bf16[24,4096]{1,0:T(8,128)(2,1)S(1)}, u32[]{:S(2)}, u32[]{:S(2)}) collective-permute-start(bf16[24,4096]{1,0:T(8,128)(2,1)S(1)} %attend.3.refs_0_), channel_id=1, source_target_pairs={{0,8},{2,10},{4,0},{6,2},{8,12},{10,14},{12,4},{14,6},{1,9},{3,11}... | collective-permute-start | bytes 589832 | tf_op jit(solution)/shard_map/ppermute | solution.py:42
  9.4 0.7 fusion.2
  10.1 3.4 %all-to-all-start = ((bf16[8,24,640]{2,1,0:T(8,128)(2,1)}), bf16[8,24,640]{2,1,0:T(8,128)(2,1)S(1)}, u32[]{:S(2)}, u32[]{:S(2)}) async-start(bf16[8,24,640]{2,1,0:T(8,128)(2,1)} %fusion.2), calls=%async_computation | async-start | bytes 491520 | tf_op jit(solution)/shard_map/all_to_all | solution.py:514
  13.6 4.7 %attend.2.refs_0_ = bf16[24,4096]{1,0:T(8,128)(2,1)S(1)} custom-call(s32[1]{0:T(128)} %bitcast.4.tab_ref, s32[48]{0:T(128)} %len_ref.3, bf16[2,24,4096]{2,1,0:T(8,128)(2,1)} %bitcast.47, bf16[2,24,2,256]{3,2,1,0:T(2,128)(2,1)} %bitcast.50, bf16[48,2,128,256]{3,2,1,0:T(8,128)(2,1)} %cache_ref.3), custom_call_target="tpu_custom_call" | custom-call | tf_op jit(solution)/shard_map/attend/pallas_call | solution.py:166
  18.3 2.0 %collective-permute-start.2 = (bf16[24,4096]{1,0:T(8,128)(2,1)S(1)}, bf16[24,4096]{1,0:T(8,128)(2,1)S(1)}, u32[]{:S(2)}, u32[]{:S(2)}) collective-permute-start(bf16[24,4096]{1,0:T(8,128)(2,1)S(1)} %attend.2.refs_0_), channel_id=1, source_target_pairs={{0,4},{2,6},{4,12},{6,14},{8,0},{10,2},{12,8},{14,10},{1,5},{3,7},... | collective-permute-start | bytes 589832 | tf_op jit(solution)/shard_map/ppermute | solution.py:42
  20.3 1.0 collective-permute-start
  21.3 1.4 %collective-permute-start.9 = (bf16[24,4096]{1,0:T(8,128)(2,1)S(1)}, bf16[24,4096]{1,0:T(8,128)(2,1)S(1)}, u32[]{:S(2)}, u32[]{:S(2)}) collective-permute-start(bf16[24,4096]{1,0:T(8,128)(2,1)S(1)} %attend.3.refs_0_), channel_id=1, source_target_pairs={{0,4},{2,6},{4,12},{6,14},{8,0},{10,2},{12,8},{14,10},{1,5},{3,7},... | collective-permute-start | bytes 589832 | tf_op jit(solution)/shard_map/ppermute | solution.py:42
  22.7 1.6 %collective-permute-start.8 = (bf16[24,4096]{1,0:T(8,128)(2,1)S(1)}, bf16[24,4096]{1,0:T(8,128)(2,1)S(1)}, u32[]{:S(2)}, u32[]{:S(2)}) collective-permute-start(bf16[24,4096]{1,0:T(8,128)(2,1)S(1)} %collective-permute-done.7.refs_1_), channel_id=1, source_target_pairs={{0,8},{2,10},{4,0},{6,2},{8,12},{10,14},{12,4},{14,6},{1,9},{3,11}... | collective-permute-start | bytes 589832 | tf_op jit(solution)/shard_map/ppermute | solution.py:42
  24.2 4.0 %collective-permute-done.2.refs_3_ = bf16[24,4096]{1,0:T(8,128)(2,1)S(1)} collective-permute-done((bf16[24,4096]{1,0:T(8,128)(2,1)S(1)}, bf16[24,4096]{1,0:T(8,128)(2,1)S(1)}, u32[]{:S(2)}, u32[]{:S(2)}) %collective-permute-start.2) | collective-permute-done | bytes 196640 | tf_op jit(solution)/shard_map/ppermute | solution.py:42
  28.3 4.4 %collective-permute-done.refs_1_ = bf16[24,4096]{1,0:T(8,128)(2,1)S(1)} collective-permute-done((bf16[24,4096]{1,0:T(8,128)(2,1)S(1)}, bf16[24,4096]{1,0:T(8,128)(2,1)S(1)}, u32[]{:S(2)}, u32[]{:S(2)}) %collective-permute-start) | collective-permute-done | bytes 196640 | tf_op jit(solution)/shard_map/ppermute | solution.py:42
  33.2 2.7 %collective-permute-done.9.refs_3_ = bf16[24,4096]{1,0:T(8,128)(2,1)S(1)} collective-permute-done((bf16[24,4096]{1,0:T(8,128)(2,1)S(1)}, bf16[24,4096]{1,0:T(8,128)(2,1)S(1)}, u32[]{:S(2)}, u32[]{:S(2)}) %collective-permute-start.9) | collective-permute-done | bytes 196640 | tf_op jit(solution)/shard_map/ppermute | solution.py:42
  35.9 3.8 %collective-permute-done.8.refs_2_ = bf16[24,4096]{1,0:T(8,128)(2,1)S(1)} collective-permute-done((bf16[24,4096]{1,0:T(8,128)(2,1)S(1)}, bf16[24,4096]{1,0:T(8,128)(2,1)S(1)}, u32[]{:S(2)}, u32[]{:S(2)}) %collective-permute-start.8) | collective-permute-done | bytes 196640 | tf_op jit(solution)/shard_map/ppermute | solution.py:42
  39.8 0.7 fusion.10
  40.5 0.7 broadcast_add_fusion
  41.2 0.5 collective-permute-start.3
  41.8 2.1 %collective-permute-done.1.refs_2_ = bf16[24,4096]{1,0:T(8,128)(2,1)S(1)} collective-permute-done((bf16[24,4096]{1,0:T(8,128)(2,1)S(1)}, bf16[24,4096]{1,0:T(8,128)(2,1)S(1)}, u32[]{:S(2)}, u32[]{:S(2)}) %collective-permute-start.1) | collective-permute-done | bytes 196640 | tf_op jit(solution)/shard_map/ppermute | solution.py:42
  44.5 3.8 %project.2 = (bf16[8,24,512]{2,1,0:T(8,128)(2,1)S(1)}, bf16[4096,512]{1,0:T(8,128)(2,1)S(1)}) custom-call(s32[14]{0:T(128)S(1)} %concatenate.13.tab_ref, bf16[24,4096]{1,0:T(8,128)(2,1)S(1)} %attend.3.refs_0_, bf16[24,4096]{1,0:T(8,128)(2,1)S(1)} %collective-permute-done.7.refs_1_, bf16[24,4096]{1,0:T(8,128)(2,1)S(1)} %collective-permute-done.8.refs_2_, ...), custom_call_target="tpu_custom_call" | custom-call | tf_op jit(solution)/shard_map/project/pallas_call | solution.py:248
  48.3 1.6 %collective-permute-start.14 = (bf16[8,24,512]{2,1,0:T(8,128)(2,1)S(1)}, bf16[8,24,512]{2,1,0:T(8,128)(2,1)S(1)}, u32[]{:S(2)}, u32[]{:S(2)}) collective-permute-start(bf16[8,24,512]{2,1,0:T(8,128)(2,1)S(1)} %get-tuple-element.30), channel_id=1, source_target_pairs={{1,0},{0,1},{3,2},{2,3},{5,4},{4,5},{7,6},{6,7},{9,8},{8,9},{11,10... | collective-permute-start | bytes 589832 | tf_op jit(solution)/shard_map/ppermute | solution.py:50
  49.8 5.7 %collective-permute-done.14.refs_9_ = bf16[8,24,512]{2,1,0:T(8,128)(2,1)S(1)} collective-permute-done((bf16[8,24,512]{2,1,0:T(8,128)(2,1)S(1)}, bf16[8,24,512]{2,1,0:T(8,128)(2,1)S(1)}, u32[]{:S(2)}, u32[]{:S(2)}) %collective-permute-start.14) | collective-permute-done | bytes 196640 | tf_op jit(solution)/shard_map/ppermute | solution.py:50
  55.6 1.6 %project.3.refs_0_ = bf16[8,24,512]{2,1,0:T(8,128)(2,1)S(1)} custom-call(s32[14]{0:T(128)S(1)} %concatenate.13.tab_ref, bf16[24,4096]{1,0:T(8,128)(2,1)S(1)} %attend.2.refs_0_, bf16[24,4096]{1,0:T(8,128)(2,1)S(1)} %collective-permute-done.refs_1_, bf16[24,4096]{1,0:T(8,128)(2,1)S(1)} %collective-permute-done.1.refs_2_, ...), custom_call_target="tpu_custom_call" | custom-call | tf_op jit(solution)/shard_map/project/pallas_call | solution.py:248
  57.1 1.3 collective-permute-start.15
  58.4 1.5 %collective-permute-start.22 = (bf16[8,24,512]{2,1,0:T(8,128)(2,1)S(1)}, bf16[8,24,512]{2,1,0:T(8,128)(2,1)S(1)}, u32[]{:S(2)}, u32[]{:S(2)}) collective-permute-start(bf16[8,24,512]{2,1,0:T(8,128)(2,1)S(1)} %project.3.refs_0_), channel_id=1, source_target_pairs={{1,0},{0,1},{3,2},{2,3},{5,4},{4,5},{7,6},{6,7},{9,8},{8,9},{11,10... | collective-permute-start | bytes 589832 | tf_op jit(solution)/shard_map/ppermute | solution.py:50
  59.9 1.1 collective-permute-start.17
  61.0 2.7 %collective-permute-done.15.refs_1_ = bf16[8,24,512]{2,1,0:T(8,128)(2,1)S(1)} collective-permute-done((bf16[8,24,512]{2,1,0:T(8,128)(2,1)S(1)}, bf16[8,24,512]{2,1,0:T(8,128)(2,1)S(1)}, u32[]{:S(2)}, u32[]{:S(2)}) %collective-permute-start.15) | collective-permute-done | bytes 196640 | tf_op jit(solution)/shard_map/ppermute | solution.py:42
  63.7 7.3 %collective-permute-start.16 = (bf16[8,24,512]{2,1,0:T(8,128)(2,1)S(1)}, bf16[8,24,512]{2,1,0:T(8,128)(2,1)S(1)}, u32[]{:S(2)}, u32[]{:S(2)}) collective-permute-start(bf16[8,24,512]{2,1,0:T(8,128)(2,1)S(1)} %collective-permute-done.15.refs_1_), channel_id=1, source_target_pairs={{0,8},{2,10},{4,0},{6,2},{8,12},{10,14},{12,4},{14,6},{1,9},{3,11}... | collective-permute-start | bytes 589832 | tf_op jit(solution)/shard_map/ppermute | solution.py:42
  71.0 1.3 collective-permute-done.17.refs_3_
  72.4 1.9 %collective-permute-start.23 = (bf16[8,24,512]{2,1,0:T(8,128)(2,1)S(1)}, bf16[8,24,512]{2,1,0:T(8,128)(2,1)S(1)}, u32[]{:S(2)}, u32[]{:S(2)}) collective-permute-start(bf16[8,24,512]{2,1,0:T(8,128)(2,1)S(1)} %collective-permute-done.15.refs_1_), channel_id=1, source_target_pairs={{1,0},{0,1},{3,2},{2,3},{5,4},{4,5},{7,6},{6,7},{9,8},{8,9},{11,10... | collective-permute-start | bytes 589832 | tf_op jit(solution)/shard_map/ppermute | solution.py:50
  74.3 1.5 %collective-permute-start.26 = (bf16[8,24,512]{2,1,0:T(8,128)(2,1)S(1)}, bf16[8,24,512]{2,1,0:T(8,128)(2,1)S(1)}, u32[]{:S(2)}, u32[]{:S(2)}) collective-permute-start(bf16[8,24,512]{2,1,0:T(8,128)(2,1)S(1)} %collective-permute-done.16.refs_2_), channel_id=1, source_target_pairs={{1,0},{0,1},{3,2},{2,3},{5,4},{4,5},{7,6},{6,7},{9,8},{8,9},{11,10... | collective-permute-start | bytes 589832 | tf_op jit(solution)/shard_map/ppermute | solution.py:50
  75.9 4.2 %collective-permute-done.27.refs_1_ = bf16[8,24,512]{2,1,0:T(8,128)(2,1)S(1)} collective-permute-done((bf16[8,24,512]{2,1,0:T(8,128)(2,1)S(1)}, bf16[8,24,512]{2,1,0:T(8,128)(2,1)S(1)}, u32[]{:S(2)}, u32[]{:S(2)}) %collective-permute-start.27) | collective-permute-done | bytes 196640 | tf_op jit(solution)/shard_map/ppermute | solution.py:50
  80.1 0.5 collective-permute-start.29
  80.6 3.7 %collective-permute-done.23.refs_9_ = bf16[8,24,512]{2,1,0:T(8,128)(2,1)S(1)} collective-permute-done((bf16[8,24,512]{2,1,0:T(8,128)(2,1)S(1)}, bf16[8,24,512]{2,1,0:T(8,128)(2,1)S(1)}, u32[]{:S(2)}, u32[]{:S(2)}) %collective-permute-start.23) | collective-permute-done | bytes 196640 | tf_op jit(solution)/shard_map/ppermute | solution.py:50
  84.3 2.6 %collective-permute-done.26.refs_0_ = bf16[8,24,512]{2,1,0:T(8,128)(2,1)S(1)} collective-permute-done((bf16[8,24,512]{2,1,0:T(8,128)(2,1)S(1)}, bf16[8,24,512]{2,1,0:T(8,128)(2,1)S(1)}, u32[]{:S(2)}, u32[]{:S(2)}) %collective-permute-start.26) | collective-permute-done | bytes 196640 | tf_op jit(solution)/shard_map/ppermute | solution.py:50
  87.2 7.3 %expert_up.2 = (bf16[2,4,2,24,384]{4,3,2,1,0:T(8,128)(2,1)S(1)}, f32[4,192,384]{2,1,0:T(8,128)S(1)}, f32[192,1]{1,0:T(8,128)S(1)}, bf16[24,4096]{1,0:T(8,128)(2,...) custom-call(s32[14]{0:T(128)S(1)} %concatenate.13.tab_ref, ...), custom_call_target="tpu_custom_call" | custom-call | tf_op jit(solution)/shard_map/expert_up/pallas_call | solution.py:432
  94.6 4.7 %expert_up.3 = (bf16[2,4,24,2048]{3,2,1,0:T(8,128)(2,1)S(1)}, bf16[2,4,24,2048]{3,2,1,0:T(8,128)(2,1)S(1)}, bf16[2,4,24,2048]{3,2,1,0:T(8,128)(2,1)S(1)}, bf16[2,4,24,2048]{3,2,1,0:T(8,128)(2,1)S(1)}) custom-call(s32[14]{0:T(128)S(1)} %concatenate.13.tab_ref, bf16[8,24,512]{2,1,0:T(8,128)(2,1)S(1)} %collective-permute-done.26.refs_0_, ...), custom_call_target="tpu_custom_call" | custom-call | tf_op jit(solution)/shard_map/expert_up/pallas_call | solution.py:432
  99.3 0.6 collective-permute-start.35
  100.0 1.8 %collective-permute-done.35.refs_1_ = bf16[2,4,24,2048]{3,2,1,0:T(8,128)(2,1)S(1)} collective-permute-done((bf16[2,4,24,2048]{3,2,1,0:T(8,128)(2,1)S(1)}, bf16[2,4,24,2048]{3,2,1,0:T(8,128)(2,1)S(1)}, u32[]{:S(2)}, u32[]{:S(2)}) %collective-permute-start.35) | collective-permute-done | bytes 786464 | tf_op jit(solution)/shard_map/ppermute | solution.py:46
  102.0 1.0 collective-permute-start.36
  103.2 2.5 %collective-permute-start.31 = (bf16[2,24,2048]{2,1,0:T(8,128)(2,1)S(1)}, bf16[2,24,2048]{2,1,0:T(8,128)(2,1)S(1)}, u32[]{:S(2)}, u32[]{:S(2)}) collective-permute-start(bf16[2,24,2048]{2,1,0:T(8,128)(2,1)S(1)} %get-tuple-element.42), channel_id=1, source_target_pairs={{0,8},{2,10},{4,0},{6,2},{8,12},{10,14},{12,4},{14,6},{1,9},{3,11}... | collective-permute-start | bytes 589832 | tf_op jit(solution)/shard_map/ppermute | solution.py:42
  105.7 5.3 %collective-permute-done.31.refs_1_ = bf16[2,24,2048]{2,1,0:T(8,128)(2,1)S(1)} collective-permute-done((bf16[2,24,2048]{2,1,0:T(8,128)(2,1)S(1)}, bf16[2,24,2048]{2,1,0:T(8,128)(2,1)S(1)}, u32[]{:S(2)}, u32[]{:S(2)}) %collective-permute-start.31) | collective-permute-done | bytes 196640 | tf_op jit(solution)/shard_map/ppermute | solution.py:42
  111.1 3.4 %collective-permute-start.32 = (bf16[2,24,2048]{2,1,0:T(8,128)(2,1)S(1)}, bf16[2,24,2048]{2,1,0:T(8,128)(2,1)S(1)}, u32[]{:S(2)}, u32[]{:S(2)}) collective-permute-start(bf16[2,24,2048]{2,1,0:T(8,128)(2,1)S(1)} %add.102), channel_id=1, source_target_pairs={{0,8},{2,10},{4,0},{6,2},{8,12},{10,14},{12,4},{14,6},{1,9},{3,11}... | collective-permute-start | bytes 589832 | tf_op jit(solution)/shard_map/ppermute | solution.py:42
  114.6 1.5 %collective-permute-start.37 = (bf16[24,2048]{1,0:T(8,128)(2,1)S(1)}, bf16[24,2048]{1,0:T(8,128)(2,1)S(1)}, u32[]{:S(2)}, u32[]{:S(2)}) collective-permute-start(bf16[24,2048]{1,0:T(8,128)(2,1)S(1)} %get-tuple-element.50), channel_id=1, source_target_pairs={{0,8},{2,10},{4,0},{6,2},{8,12},{10,14},{12,4},{14,6},{1,9},{3,11}... | collective-permute-start | bytes 294920 | tf_op jit(solution)/shard_map/ppermute | solution.py:42
  116.0 3.8 %collective-permute-done.32 = bf16[2,24,2048]{2,1,0:T(8,128)(2,1)S(1)} collective-permute-done((bf16[2,24,2048]{2,1,0:T(8,128)(2,1)S(1)}, bf16[2,24,2048]{2,1,0:T(8,128)(2,1)S(1)}, u32[]{:S(2)}, u32[]{:S(2)}) %collective-permute-start.32) | collective-permute-done | bytes 196640 | tf_op jit(solution)/shard_map/ppermute | solution.py:42
  119.9 1.1 collective-permute-start.34
  120.9 0.7 collective-permute-start.39
  121.8 3.4 %collective-permute-start.38 = (bf16[24,2048]{1,0:T(8,128)(2,1)S(1)}, bf16[24,2048]{1,0:T(8,128)(2,1)S(1)}, u32[]{:S(2)}, u32[]{:S(2)}) collective-permute-start(bf16[24,2048]{1,0:T(8,128)(2,1)S(1)} %add.105), channel_id=1, source_target_pairs={{0,8},{2,10},{4,0},{6,2},{8,12},{10,14},{12,4},{14,6},{1,9},{3,11}... | collective-permute-start | bytes 294920 | tf_op jit(solution)/shard_map/ppermute | solution.py:42
  125.3 2.4 %collective-permute-done.39 = bf16[24,2048]{1,0:T(8,128)(2,1)S(1)} collective-permute-done((bf16[24,2048]{1,0:T(8,128)(2,1)S(1)}, bf16[24,2048]{1,0:T(8,128)(2,1)S(1)}, u32[]{:S(2)}, u32[]{:S(2)}) %collective-permute-start.39) | collective-permute-done | bytes 98336 | tf_op jit(solution)/shard_map/ppermute | solution.py:42
  127.8 0.7 fusion.1
  (76 shorter events, 3.0 us)
Async XLA Ops:
  0.0 9.0 %copy-start.2 = (f32[48,8]{0,1:T(8,128)S(1)}, f32[48,8]{0,1:T(8,128)}, u32[]{:S(2)}) copy-start(f32[48,8]{0,1:T(8,128)} %param.24) | copy-start | bytes 4612
  0.0 9.0 %copy-start.3 = (s32[48,8]{0,1:T(8,128)S(1)}, s32[48,8]{0,1:T(8,128)}, u32[]{:S(2)}) copy-start(s32[48,8]{0,1:T(8,128)} %param.23) | copy-start | bytes 4612
  0.0 9.4 %copy-start = (bf16[24,4096]{1,0:T(8,128)(2,1)S(1)}, bf16[24,4096]{1,0:T(8,128)(2,1)}, u32[]{:S(2)}) copy-start(bf16[24,4096]{1,0:T(8,128)(2,1)} %param.21) | copy-start | bytes 589828
  4.9 17.8 %collective-permute-start.7 = (bf16[24,4096]{1,0:T(8,128)(2,1)S(1)}, bf16[24,4096]{1,0:T(8,128)(2,1)S(1)}, u32[]{:S(2)}, u32[]{:S(2)}) collective-permute-start(bf16[24,4096]{1,0:T(8,128)(2,1)S(1)} %attend.3.refs_0_), channel_id=1, source_target_pairs={{0,8},{2,10},{4,0},{6,2},{8,12},{10,14},{12,4},{14,6},{1,9},{3,11}... | collective-permute-start | bytes 589832 | tf_op jit(solution)/shard_map/ppermute | solution.py:42
  10.1 34.4 %all-to-all-start = ((bf16[8,24,640]{2,1,0:T(8,128)(2,1)}), bf16[8,24,640]{2,1,0:T(8,128)(2,1)S(1)}, u32[]{:S(2)}, u32[]{:S(2)}) async-start(bf16[8,24,640]{2,1,0:T(8,128)(2,1)} %fusion.2), calls=%async_computation | async-start | bytes 491520 | tf_op jit(solution)/shard_map/all_to_all | solution.py:514
  18.3 57.5 %copy-start.1 = (bf16[4096]{0:T(1024)(128)(2,1)S(1)}, bf16[4096]{0:T(1024)(128)(2,1)}, u32[]{:S(2)}) copy-start(bf16[4096]{0:T(1024)(128)(2,1)} %param.22) | copy-start | bytes 24580
  18.3 9.9 %collective-permute-start.2 = (bf16[24,4096]{1,0:T(8,128)(2,1)S(1)}, bf16[24,4096]{1,0:T(8,128)(2,1)S(1)}, u32[]{:S(2)}, u32[]{:S(2)}) collective-permute-start(bf16[24,4096]{1,0:T(8,128)(2,1)S(1)} %attend.2.refs_0_), channel_id=1, source_target_pairs={{0,4},{2,6},{4,12},{6,14},{8,0},{10,2},{12,8},{14,10},{1,5},{3,7},... | collective-permute-start | bytes 589832 | tf_op jit(solution)/shard_map/ppermute | solution.py:42
  20.3 12.4 %collective-permute-start = (bf16[24,4096]{1,0:T(8,128)(2,1)S(1)}, bf16[24,4096]{1,0:T(8,128)(2,1)S(1)}, u32[]{:S(2)}, u32[]{:S(2)}) collective-permute-start(bf16[24,4096]{1,0:T(8,128)(2,1)S(1)} %attend.2.refs_0_), channel_id=1, source_target_pairs={{0,8},{2,10},{4,0},{6,2},{8,12},{10,14},{12,4},{14,6},{1,9},{3,11}... | collective-permute-start | bytes 589832 | tf_op jit(solution)/shard_map/ppermute | solution.py:42
  21.3 14.6 %collective-permute-start.9 = (bf16[24,4096]{1,0:T(8,128)(2,1)S(1)}, bf16[24,4096]{1,0:T(8,128)(2,1)S(1)}, u32[]{:S(2)}, u32[]{:S(2)}) collective-permute-start(bf16[24,4096]{1,0:T(8,128)(2,1)S(1)} %attend.3.refs_0_), channel_id=1, source_target_pairs={{0,4},{2,6},{4,12},{6,14},{8,0},{10,2},{12,8},{14,10},{1,5},{3,7},... | collective-permute-start | bytes 589832 | tf_op jit(solution)/shard_map/ppermute | solution.py:42
  22.7 17.1 %collective-permute-start.8 = (bf16[24,4096]{1,0:T(8,128)(2,1)S(1)}, bf16[24,4096]{1,0:T(8,128)(2,1)S(1)}, u32[]{:S(2)}, u32[]{:S(2)}) collective-permute-start(bf16[24,4096]{1,0:T(8,128)(2,1)S(1)} %collective-permute-done.7.refs_1_), channel_id=1, source_target_pairs={{0,8},{2,10},{4,0},{6,2},{8,12},{10,14},{12,4},{14,6},{1,9},{3,11}... | collective-permute-start | bytes 589832 | tf_op jit(solution)/shard_map/ppermute | solution.py:42
  24.2 17.0 %collective-permute-start.10 = (bf16[24,4096]{1,0:T(8,128)(2,1)S(1)}, bf16[24,4096]{1,0:T(8,128)(2,1)S(1)}, u32[]{:S(2)}, u32[]{:S(2)}) collective-permute-start(bf16[24,4096]{1,0:T(8,128)(2,1)S(1)} %attend.3.refs_0_), channel_id=1, source_target_pairs={{0,2},{2,0},{4,6},{6,4},{8,10},{10,8},{12,14},{14,12},{1,3},{3,1},... | collective-permute-start | bytes 589832 | tf_op jit(solution)/shard_map/ppermute | solution.py:46
  28.3 16.2 %collective-permute-start.11 = (bf16[24,4096]{1,0:T(8,128)(2,1)S(1)}, bf16[24,4096]{1,0:T(8,128)(2,1)S(1)}, u32[]{:S(2)}, u32[]{:S(2)}) collective-permute-start(bf16[24,4096]{1,0:T(8,128)(2,1)S(1)} %collective-permute-done.7.refs_1_), channel_id=1, source_target_pairs={{0,2},{2,0},{4,6},{6,4},{8,10},{10,8},{12,14},{14,12},{1,3},{3,1},... | collective-permute-start | bytes 589832 | tf_op jit(solution)/shard_map/ppermute | solution.py:46
  32.7 11.2 %collective-permute-start.1 = (bf16[24,4096]{1,0:T(8,128)(2,1)S(1)}, bf16[24,4096]{1,0:T(8,128)(2,1)S(1)}, u32[]{:S(2)}, u32[]{:S(2)}) collective-permute-start(bf16[24,4096]{1,0:T(8,128)(2,1)S(1)} %collective-permute-done.refs_1_), channel_id=1, source_target_pairs={{0,8},{2,10},{4,0},{6,2},{8,12},{10,14},{12,4},{14,6},{1,9},{3,11}... | collective-permute-start | bytes 589832 | tf_op jit(solution)/shard_map/ppermute | solution.py:42
  35.9 8.0 %collective-permute-start.13 = (bf16[24,4096]{1,0:T(8,128)(2,1)S(1)}, bf16[24,4096]{1,0:T(8,128)(2,1)S(1)}, u32[]{:S(2)}, u32[]{:S(2)}) collective-permute-start(bf16[24,4096]{1,0:T(8,128)(2,1)S(1)} %collective-permute-done.9.refs_3_), channel_id=1, source_target_pairs={{0,2},{2,0},{4,6},{6,4},{8,10},{10,8},{12,14},{14,12},{1,3},{3,1},... | collective-permute-start | bytes 589832 | tf_op jit(solution)/shard_map/ppermute | solution.py:46
  39.8 4.7 %collective-permute-start.12 = (bf16[24,4096]{1,0:T(8,128)(2,1)S(1)}, bf16[24,4096]{1,0:T(8,128)(2,1)S(1)}, u32[]{:S(2)}, u32[]{:S(2)}) collective-permute-start(bf16[24,4096]{1,0:T(8,128)(2,1)S(1)} %collective-permute-done.8.refs_2_), channel_id=1, source_target_pairs={{0,2},{2,0},{4,6},{6,4},{8,10},{10,8},{12,14},{14,12},{1,3},{3,1},... | collective-permute-start | bytes 589832 | tf_op jit(solution)/shard_map/ppermute | solution.py:46
  41.2 8.6 %collective-permute-start.3 = (bf16[24,4096]{1,0:T(8,128)(2,1)S(1)}, bf16[24,4096]{1,0:T(8,128)(2,1)S(1)}, u32[]{:S(2)}, u32[]{:S(2)}) collective-permute-start(bf16[24,4096]{1,0:T(8,128)(2,1)S(1)} %attend.2.refs_0_), channel_id=1, source_target_pairs={{0,2},{2,0},{4,6},{6,4},{8,10},{10,8},{12,14},{14,12},{1,3},{3,1},... | collective-permute-start | bytes 589832 | tf_op jit(solution)/shard_map/ppermute | solution.py:46
  43.9 5.9 %collective-permute-start.4 = (bf16[24,4096]{1,0:T(8,128)(2,1)S(1)}, bf16[24,4096]{1,0:T(8,128)(2,1)S(1)}, u32[]{:S(2)}, u32[]{:S(2)}) collective-permute-start(bf16[24,4096]{1,0:T(8,128)(2,1)S(1)} %collective-permute-done.refs_1_), channel_id=1, source_target_pairs={{0,2},{2,0},{4,6},{6,4},{8,10},{10,8},{12,14},{14,12},{1,3},{3,1},... | collective-permute-start | bytes 589832 | tf_op jit(solution)/shard_map/ppermute | solution.py:46
  43.9 5.9 %collective-permute-start.6 = (bf16[24,4096]{1,0:T(8,128)(2,1)S(1)}, bf16[24,4096]{1,0:T(8,128)(2,1)S(1)}, u32[]{:S(2)}, u32[]{:S(2)}) collective-permute-start(bf16[24,4096]{1,0:T(8,128)(2,1)S(1)} %collective-permute-done.2.refs_3_), channel_id=1, source_target_pairs={{0,2},{2,0},{4,6},{6,4},{8,10},{10,8},{12,14},{14,12},{1,3},{3,1},... | collective-permute-start | bytes 589832 | tf_op jit(solution)/shard_map/ppermute | solution.py:46
  44.4 5.4 %collective-permute-start.5 = (bf16[24,4096]{1,0:T(8,128)(2,1)S(1)}, bf16[24,4096]{1,0:T(8,128)(2,1)S(1)}, u32[]{:S(2)}, u32[]{:S(2)}) collective-permute-start(bf16[24,4096]{1,0:T(8,128)(2,1)S(1)} %collective-permute-done.1.refs_2_), channel_id=1, source_target_pairs={{0,2},{2,0},{4,6},{6,4},{8,10},{10,8},{12,14},{14,12},{1,3},{3,1},... | collective-permute-start | bytes 589832 | tf_op jit(solution)/shard_map/ppermute | solution.py:46
  48.3 7.3 %collective-permute-start.14 = (bf16[8,24,512]{2,1,0:T(8,128)(2,1)S(1)}, bf16[8,24,512]{2,1,0:T(8,128)(2,1)S(1)}, u32[]{:S(2)}, u32[]{:S(2)}) collective-permute-start(bf16[8,24,512]{2,1,0:T(8,128)(2,1)S(1)} %get-tuple-element.30), channel_id=1, source_target_pairs={{1,0},{0,1},{3,2},{2,3},{5,4},{4,5},{7,6},{6,7},{9,8},{8,9},{11,10... | collective-permute-start | bytes 589832 | tf_op jit(solution)/shard_map/ppermute | solution.py:50
  57.1 6.6 %collective-permute-start.15 = (bf16[8,24,512]{2,1,0:T(8,128)(2,1)S(1)}, bf16[8,24,512]{2,1,0:T(8,128)(2,1)S(1)}, u32[]{:S(2)}, u32[]{:S(2)}) collective-permute-start(bf16[8,24,512]{2,1,0:T(8,128)(2,1)S(1)} %project.3.refs_0_), channel_id=1, source_target_pairs={{0,8},{2,10},{4,0},{6,2},{8,12},{10,14},{12,4},{14,6},{1,9},{3,11}... | collective-permute-start | bytes 589832 | tf_op jit(solution)/shard_map/ppermute | solution.py:42
  58.4 12.6 %collective-permute-start.22 = (bf16[8,24,512]{2,1,0:T(8,128)(2,1)S(1)}, bf16[8,24,512]{2,1,0:T(8,128)(2,1)S(1)}, u32[]{:S(2)}, u32[]{:S(2)}) collective-permute-start(bf16[8,24,512]{2,1,0:T(8,128)(2,1)S(1)} %project.3.refs_0_), channel_id=1, source_target_pairs={{1,0},{0,1},{3,2},{2,3},{5,4},{4,5},{7,6},{6,7},{9,8},{8,9},{11,10... | collective-permute-start | bytes 589832 | tf_op jit(solution)/shard_map/ppermute | solution.py:50
  59.9 12.4 %collective-permute-start.17 = (bf16[8,24,512]{2,1,0:T(8,128)(2,1)S(1)}, bf16[8,24,512]{2,1,0:T(8,128)(2,1)S(1)}, u32[]{:S(2)}, u32[]{:S(2)}) collective-permute-start(bf16[8,24,512]{2,1,0:T(8,128)(2,1)S(1)} %project.3.refs_0_), channel_id=1, source_target_pairs={{0,4},{2,6},{4,12},{6,14},{8,0},{10,2},{12,8},{14,10},{1,5},{3,7},... | collective-permute-start | bytes 589832 | tf_op jit(solution)/shard_map/ppermute | solution.py:42
  61.0 11.4 %collective-permute-start.18 = (bf16[8,24,512]{2,1,0:T(8,128)(2,1)S(1)}, bf16[8,24,512]{2,1,0:T(8,128)(2,1)S(1)}, u32[]{:S(2)}, u32[]{:S(2)}) collective-permute-start(bf16[8,24,512]{2,1,0:T(8,128)(2,1)S(1)} %project.3.refs_0_), channel_id=1, source_target_pairs={{0,2},{2,0},{4,6},{6,4},{8,10},{10,8},{12,14},{14,12},{1,3},{3,1},... | collective-permute-start | bytes 589832 | tf_op jit(solution)/shard_map/ppermute | solution.py:46
  63.7 10.6 %collective-permute-start.16 = (bf16[8,24,512]{2,1,0:T(8,128)(2,1)S(1)}, bf16[8,24,512]{2,1,0:T(8,128)(2,1)S(1)}, u32[]{:S(2)}, u32[]{:S(2)}) collective-permute-start(bf16[8,24,512]{2,1,0:T(8,128)(2,1)S(1)} %collective-permute-done.15.refs_1_), channel_id=1, source_target_pairs={{0,8},{2,10},{4,0},{6,2},{8,12},{10,14},{12,4},{14,6},{1,9},{3,11}... | collective-permute-start | bytes 589832 | tf_op jit(solution)/shard_map/ppermute | solution.py:42
  71.0 4.8 %collective-permute-start.24 = (bf16[8,24,512]{2,1,0:T(8,128)(2,1)S(1)}, bf16[8,24,512]{2,1,0:T(8,128)(2,1)S(1)}, u32[]{:S(2)}, u32[]{:S(2)}) collective-permute-start(bf16[8,24,512]{2,1,0:T(8,128)(2,1)S(1)} %collective-permute-done.22.refs_8_), channel_id=1, source_target_pairs={{0,2},{2,0},{4,6},{6,4},{8,10},{10,8},{12,14},{14,12},{1,3},{3,1},... | collective-permute-start | bytes 589832 | tf_op jit(solution)/shard_map/ppermute | solution.py:46
  72.3 7.8 %collective-permute-start.27 = (bf16[8,24,512]{2,1,0:T(8,128)(2,1)S(1)}, bf16[8,24,512]{2,1,0:T(8,128)(2,1)S(1)}, u32[]{:S(2)}, u32[]{:S(2)}) collective-permute-start(bf16[8,24,512]{2,1,0:T(8,128)(2,1)S(1)} %collective-permute-done.17.refs_3_), channel_id=1, source_target_pairs={{1,0},{0,1},{3,2},{2,3},{5,4},{4,5},{7,6},{6,7},{9,8},{8,9},{11,10... | collective-permute-start | bytes 589832 | tf_op jit(solution)/shard_map/ppermute | solution.py:50
  72.4 7.7 %collective-permute-start.21 = (bf16[8,24,512]{2,1,0:T(8,128)(2,1)S(1)}, bf16[8,24,512]{2,1,0:T(8,128)(2,1)S(1)}, u32[]{:S(2)}, u32[]{:S(2)}) collective-permute-start(bf16[8,24,512]{2,1,0:T(8,128)(2,1)S(1)} %collective-permute-done.17.refs_3_), channel_id=1, source_target_pairs={{0,2},{2,0},{4,6},{6,4},{8,10},{10,8},{12,14},{14,12},{1,3},{3,1},... | collective-permute-start | bytes 589832 | tf_op jit(solution)/shard_map/ppermute | solution.py:46
  72.4 11.9 %collective-permute-start.23 = (bf16[8,24,512]{2,1,0:T(8,128)(2,1)S(1)}, bf16[8,24,512]{2,1,0:T(8,128)(2,1)S(1)}, u32[]{:S(2)}, u32[]{:S(2)}) collective-permute-start(bf16[8,24,512]{2,1,0:T(8,128)(2,1)S(1)} %collective-permute-done.15.refs_1_), channel_id=1, source_target_pairs={{1,0},{0,1},{3,2},{2,3},{5,4},{4,5},{7,6},{6,7},{9,8},{8,9},{11,10... | collective-permute-start | bytes 589832 | tf_op jit(solution)/shard_map/ppermute | solution.py:50
  74.3 12.6 %collective-permute-start.26 = (bf16[8,24,512]{2,1,0:T(8,128)(2,1)S(1)}, bf16[8,24,512]{2,1,0:T(8,128)(2,1)S(1)}, u32[]{:S(2)}, u32[]{:S(2)}) collective-permute-start(bf16[8,24,512]{2,1,0:T(8,128)(2,1)S(1)} %collective-permute-done.16.refs_2_), channel_id=1, source_target_pairs={{1,0},{0,1},{3,2},{2,3},{5,4},{4,5},{7,6},{6,7},{9,8},{8,9},{11,10... | collective-permute-start | bytes 589832 | tf_op jit(solution)/shard_map/ppermute | solution.py:50
  75.8 11.4 %collective-permute-start.19 = (bf16[8,24,512]{2,1,0:T(8,128)(2,1)S(1)}, bf16[8,24,512]{2,1,0:T(8,128)(2,1)S(1)}, u32[]{:S(2)}, u32[]{:S(2)}) collective-permute-start(bf16[8,24,512]{2,1,0:T(8,128)(2,1)S(1)} %collective-permute-done.15.refs_1_), channel_id=1, source_target_pairs={{0,2},{2,0},{4,6},{6,4},{8,10},{10,8},{12,14},{14,12},{1,3},{3,1},... | collective-permute-start | bytes 589832 | tf_op jit(solution)/shard_map/ppermute | solution.py:46
  80.1 7.2 %collective-permute-start.20 = (bf16[8,24,512]{2,1,0:T(8,128)(2,1)S(1)}, bf16[8,24,512]{2,1,0:T(8,128)(2,1)S(1)}, u32[]{:S(2)}, u32[]{:S(2)}) collective-permute-start(bf16[8,24,512]{2,1,0:T(8,128)(2,1)S(1)} %collective-permute-done.16.refs_2_), channel_id=1, source_target_pairs={{0,2},{2,0},{4,6},{6,4},{8,10},{10,8},{12,14},{14,12},{1,3},{3,1},... | collective-permute-start | bytes 589832 | tf_op jit(solution)/shard_map/ppermute | solution.py:46
  80.1 14.5 %collective-permute-start.29 = (bf16[8,24,512]{2,1,0:T(8,128)(2,1)S(1)}, bf16[8,24,512]{2,1,0:T(8,128)(2,1)S(1)}, u32[]{:S(2)}, u32[]{:S(2)}) collective-permute-start(bf16[8,24,512]{2,1,0:T(8,128)(2,1)S(1)} %collective-permute-done.27.refs_1_), channel_id=1, source_target_pairs={{0,2},{2,0},{4,6},{6,4},{8,10},{10,8},{12,14},{14,12},{1,3},{3,1},... | collective-permute-start | bytes 589832 | tf_op jit(solution)/shard_map/ppermute | solution.py:46
  84.3 2.9 %collective-permute-start.25 = (bf16[8,24,512]{2,1,0:T(8,128)(2,1)S(1)}, bf16[8,24,512]{2,1,0:T(8,128)(2,1)S(1)}, u32[]{:S(2)}, u32[]{:S(2)}) collective-permute-start(bf16[8,24,512]{2,1,0:T(8,128)(2,1)S(1)} %collective-permute-done.23.refs_9_), channel_id=1, source_target_pairs={{0,2},{2,0},{4,6},{6,4},{8,10},{10,8},{12,14},{14,12},{1,3},{3,1},... | collective-permute-start | bytes 589832 | tf_op jit(solution)/shard_map/ppermute | solution.py:46
  86.9 7.7 %collective-permute-start.28 = (bf16[8,24,512]{2,1,0:T(8,128)(2,1)S(1)}, bf16[8,24,512]{2,1,0:T(8,128)(2,1)S(1)}, u32[]{:S(2)}, u32[]{:S(2)}) collective-permute-start(bf16[8,24,512]{2,1,0:T(8,128)(2,1)S(1)} %collective-permute-done.26.refs_0_), channel_id=1, source_target_pairs={{0,2},{2,0},{4,6},{6,4},{8,10},{10,8},{12,14},{14,12},{1,3},{3,1},... | collective-permute-start | bytes 589832 | tf_op jit(solution)/shard_map/ppermute | solution.py:46
  99.3 2.5 %collective-permute-start.35 = (bf16[2,4,24,2048]{3,2,1,0:T(8,128)(2,1)S(1)}, bf16[2,4,24,2048]{3,2,1,0:T(8,128)(2,1)S(1)}, u32[]{:S(2)}, u32[]{:S(2)}) collective-permute-start(bf16[2,4,24,2048]{3,2,1,0:T(8,128)(2,1)S(1)} %get-tuple-element.45), channel_id=1, source_target_pairs={{0,2},{2,0},{4,6},{6,4},{8,10},{10,8},{12,14},{14,12},{1,3},{3,1},... | collective-permute-start | bytes 2359304 | tf_op jit(solution)/shard_map/ppermute | solution.py:46
  99.9 3.1 %collective-permute-start.30 = (bf16[2,4,24,2048]{3,2,1,0:T(8,128)(2,1)S(1)}, bf16[2,4,24,2048]{3,2,1,0:T(8,128)(2,1)S(1)}, u32[]{:S(2)}, u32[]{:S(2)}) collective-permute-start(bf16[2,4,24,2048]{3,2,1,0:T(8,128)(2,1)S(1)} %get-tuple-element.39), channel_id=1, source_target_pairs={{0,2},{2,0},{4,6},{6,4},{8,10},{10,8},{12,14},{14,12},{1,3},{3,1},... | collective-permute-start | bytes 2359304 | tf_op jit(solution)/shard_map/ppermute | solution.py:46
  102.0 12.5 %collective-permute-start.36 = (bf16[4,24,2048]{2,1,0:T(8,128)(2,1)S(1)}, bf16[4,24,2048]{2,1,0:T(8,128)(2,1)S(1)}, u32[]{:S(2)}, u32[]{:S(2)}) collective-permute-start(bf16[4,24,2048]{2,1,0:T(8,128)(2,1)S(1)} %get-tuple-element.47), channel_id=1, source_target_pairs={{1,0},{0,1},{3,2},{2,3},{5,4},{4,5},{7,6},{6,7},{9,8},{8,9},{11,10... | collective-permute-start | bytes 1179656 | tf_op jit(solution)/shard_map/ppermute | solution.py:50
  103.2 7.9 %collective-permute-start.31 = (bf16[2,24,2048]{2,1,0:T(8,128)(2,1)S(1)}, bf16[2,24,2048]{2,1,0:T(8,128)(2,1)S(1)}, u32[]{:S(2)}, u32[]{:S(2)}) collective-permute-start(bf16[2,24,2048]{2,1,0:T(8,128)(2,1)S(1)} %get-tuple-element.42), channel_id=1, source_target_pairs={{0,8},{2,10},{4,0},{6,2},{8,12},{10,14},{12,4},{14,6},{1,9},{3,11}... | collective-permute-start | bytes 589832 | tf_op jit(solution)/shard_map/ppermute | solution.py:42
  105.7 10.4 %collective-permute-start.33 = (bf16[2,24,2048]{2,1,0:T(8,128)(2,1)S(1)}, bf16[2,24,2048]{2,1,0:T(8,128)(2,1)S(1)}, u32[]{:S(2)}, u32[]{:S(2)}) collective-permute-start(bf16[2,24,2048]{2,1,0:T(8,128)(2,1)S(1)} %get-tuple-element.43), channel_id=1, source_target_pairs={{0,4},{2,6},{4,12},{6,14},{8,0},{10,2},{12,8},{14,10},{1,5},{3,7},... | collective-permute-start | bytes 589832 | tf_op jit(solution)/shard_map/ppermute | solution.py:42
  111.1 8.7 %collective-permute-start.32 = (bf16[2,24,2048]{2,1,0:T(8,128)(2,1)S(1)}, bf16[2,24,2048]{2,1,0:T(8,128)(2,1)S(1)}, u32[]{:S(2)}, u32[]{:S(2)}) collective-permute-start(bf16[2,24,2048]{2,1,0:T(8,128)(2,1)S(1)} %add.102), channel_id=1, source_target_pairs={{0,8},{2,10},{4,0},{6,2},{8,12},{10,14},{12,4},{14,6},{1,9},{3,11}... | collective-permute-start | bytes 589832 | tf_op jit(solution)/shard_map/ppermute | solution.py:42
  114.6 7.2 %collective-permute-start.37 = (bf16[24,2048]{1,0:T(8,128)(2,1)S(1)}, bf16[24,2048]{1,0:T(8,128)(2,1)S(1)}, u32[]{:S(2)}, u32[]{:S(2)}) collective-permute-start(bf16[24,2048]{1,0:T(8,128)(2,1)S(1)} %get-tuple-element.50), channel_id=1, source_target_pairs={{0,8},{2,10},{4,0},{6,2},{8,12},{10,14},{12,4},{14,6},{1,9},{3,11}... | collective-permute-start | bytes 294920 | tf_op jit(solution)/shard_map/ppermute | solution.py:42
  119.9 5.4 %collective-permute-start.34 = (bf16[24,2048]{1,0:T(8,128)(2,1)S(1)}, bf16[24,2048]{1,0:T(8,128)(2,1)S(1)}, u32[]{:S(2)}, u32[]{:S(2)}) collective-permute-start(bf16[24,2048]{1,0:T(8,128)(2,1)S(1)} %fusion.4), channel_id=1, source_target_pairs={{1,0},{0,1},{3,2},{2,3},{5,4},{4,5},{7,6},{6,7},{9,8},{8,9},{11,10... | collective-permute-start | bytes 294920 | tf_op jit(solution)/shard_map/ppermute | solution.py:50
  120.9 6.8 %collective-permute-start.39 = (bf16[24,2048]{1,0:T(8,128)(2,1)S(1)}, bf16[24,2048]{1,0:T(8,128)(2,1)S(1)}, u32[]{:S(2)}, u32[]{:S(2)}) collective-permute-start(bf16[24,2048]{1,0:T(8,128)(2,1)S(1)} %get-tuple-element.51), channel_id=1, source_target_pairs={{0,4},{2,6},{4,12},{6,14},{8,0},{10,2},{12,8},{14,10},{1,5},{3,7},... | collective-permute-start | bytes 294920 | tf_op jit(solution)/shard_map/ppermute | solution.py:42
  121.8 5.9 %collective-permute-start.38 = (bf16[24,2048]{1,0:T(8,128)(2,1)S(1)}, bf16[24,2048]{1,0:T(8,128)(2,1)S(1)}, u32[]{:S(2)}, u32[]{:S(2)}) collective-permute-start(bf16[24,2048]{1,0:T(8,128)(2,1)S(1)} %add.105), channel_id=1, source_target_pairs={{0,8},{2,10},{4,0},{6,2},{8,12},{10,14},{12,4},{14,6},{1,9},{3,11}... | collective-permute-start | bytes 294920 | tf_op jit(solution)/shard_map/ppermute | solution.py:42
